TPU v7x, 256 devices: a 4x2x16 block of a 4x16x16 slice. The times are simulated.
256 devices in a mesh: win: 2 (over y), px: 128 (over x, z, core).
Axes of the slice: x: 4, y: 2, z: 16, core: 2. Of those that a mesh axis runs over, the one named last changes fastest.
The devices are a block of a 4x16x16 slice.
Arguments:
- charge_a: float32 [1048576], P(('win', 'px')), parts along dimension 0, may hold values from -3 to 3
- charge_b: float32 [1048576], P(('win', 'px')), parts along dimension 0, may hold values from -3 to 3
- coupling: float32 [2], P('win'), parts along dimension 0, may hold values from 0.1 to 0.9
- positions: float32 [3, 1048576], P(None, ('win', 'px')), parts along dimension 1, may hold values from 0 to 128, as said below
- grid_base: int32 [3, 1048576], P(None, ('win', 'px')), parts along dimension 1, may hold values from 0 to 127, as said below
- spline: float32 [3, 4, 1048576], P(None, None, ('win', 'px')), parts along dimension 2, may hold values from 0 to 0.67, as said below
- spline_slope: float32 [3, 4, 1048576], P(None, None, ('win', 'px')), parts along dimension 2, may hold values from -0.67 to 0.67, as said below
- influence: float32 [128, 128, 128], P(None, 'px'), may hold values from 0.5 to 300, as said below
- pair_tiles: int32 [8192, 12], P(('win', 'px')), parts along dimension 0, may hold values from 0 to 39
- ghost_lists: int32 [2, 131072], P(None, ('win', 'px')), parts along dimension 1, may hold values from 0 to 4095
Outputs:
- forces: float32 [3, 1048576], P(None, ('win', 'px')), parts along dimension 1
There are 2 independent parts, one for each index of `win`. A program takes and returns all parts, laid end to end along the dimension named above; an argument that names none is the same for every part. Nothing has to cross between parts.
Inputs may be any that keep to these rules, and one draw needn't show every extreme that they name: `grid_base`: row 0 of atom i lies in [d, (d + 1)) for d = i // 4096; rows 1 and 2 lie in [0, 128). `positions`: row 0 of atom i lies in [d, (d + 1)) for d = i // 4096; rows 1 and 2 lie in [0, 8). For each atom and dimension, the 4 cubic B-spline weights at some fraction u in [0, 1). `spline_slope`: the derivatives in u of the weights in spline, at the same u. influence at wave index m equals influence at -m, indices taken modulo the grid's lengths.
All inputs are finite; a program needn't handle non-finite values.
Results may differ from a plain program's by a relative error of at most 0.0003.
Values sent between devices are 32-bit elements; how exact they have to be, the bound alone decides.
A program may use at most 128 MiB of HBM per device.

v0:
```python
import math

import jax
import jax.numpy as jnp
from jax import lax
from jax.sharding import PartitionSpec as P

TILE = 128


highest = lax.Precision.HIGHEST
ewald_beta = 0.35
soften_sq = 0.25


def from_behind(value, axis, steps):
    count = lax.axis_size(axis)
    pairs = [(source, (source + steps) % count) for source in range(count)]
    return lax.ppermute(value, axis, pairs)


def dft_tables(length):
    wave_index = jnp.arange(length, dtype=jnp.int32)
    phase_angle = (
        2.0
        * math.pi
        / length
        * (wave_index[:, None] * wave_index[None, :] % length).astype(jnp.float32)
    )
    return (jnp.cos(phase_angle), jnp.sin(phase_angle))


def along_axis(values, matrix, dim_index):
    result = jnp.tensordot(values, matrix, axes=([dim_index], [0]), precision=highest)
    return jnp.moveaxis(result, -1, dim_index)


def transform(real_part, imag_part, dim_index, forward):
    cosine_table, sine_table = dft_tables(real_part.shape[dim_index])
    factor = 1.0 if forward else -1.0
    real_cos = along_axis(real_part, cosine_table, dim_index)
    real_new = real_cos + factor * along_axis(imag_part, sine_table, dim_index)
    imag_new = along_axis(imag_part, cosine_table, dim_index) - factor * along_axis(
        real_part, sine_table, dim_index
    )
    return (real_new, imag_new)


def spline_rows(base_index, weights, length, periodic):
    cell_ids = jnp.arange(length, dtype=jnp.int32)
    result = jnp.zeros((base_index.shape[0], length), jnp.float32)
    for offset in range(weights.shape[0]):
        target_cell = base_index + offset
        if periodic:
            target_cell = target_cell % length
        result = result + jnp.where(
            target_cell[:, None] == cell_ids[None, :], weights[offset][:, None], 0.0
        )
    return result


def pair_block(home_rows, nearby, weight_b):
    separation = home_rows[0:3, :, :, None] - nearby[0:3, :, None, :]
    dist_sq = jnp.sum(separation * separation, axis=0) + soften_sq
    distance = jnp.sqrt(dist_sq)
    radial = (
        jax.scipy.special.erfc(ewald_beta * distance) / distance
        + 2.0 * ewald_beta / math.sqrt(math.pi) * jnp.exp(-ewald_beta * ewald_beta * dist_sq)
    ) / dist_sq
    mixed = (1.0 - weight_b) * home_rows[3][:, :, None] * nearby[3][
        :, None, :
    ] + weight_b * home_rows[4][:, :, None] * nearby[4][:, None, :]
    return jnp.sum((mixed * radial)[None] * separation, axis=3)


def device_pairs(home_rows, candidates, tile_list, weight_b):
    home_tiles = home_rows.reshape(5, -1, TILE)
    cand_tiles = candidates.reshape(5, -1, TILE)

    def one_slot(accumulated, column):
        nearby = jnp.take(cand_tiles, column, axis=1)
        return (accumulated + pair_block(home_tiles, nearby, weight_b), None)

    start = jnp.zeros((3,) + home_tiles.shape[1:], jnp.float32)
    accumulated, unused = lax.scan(one_slot, start, tile_list.T)
    return accumulated.reshape(3, -1)


def per_device(
    charge_a,
    charge_b,
    coupling,
    positions,
    grid_base,
    spline,
    spline_slope,
    influence,
    pair_tiles,
    ghost_lists,
):
    group_size = lax.axis_size("px")
    me_index = lax.axis_index("px")
    atom_count = charge_a.shape[0]
    full_x, slab_y, full_z = influence.shape
    full_y = slab_y * group_size
    planes = full_x // group_size
    margin = spline.shape[1] - 1
    slab_width = planes + margin
    hop_count = (margin + planes - 1) // planes
    weight_b = coupling[0]
    local_x = grid_base[0] - me_index * planes
    rows_x = spline_rows(local_x, spline[0], slab_width, False)
    slope_x = spline_rows(local_x, spline_slope[0], slab_width, False)
    rows_y = spline_rows(grid_base[1], spline[1], full_y, True)
    slope_y = spline_rows(grid_base[1], spline_slope[1], full_y, True)
    rows_z = spline_rows(grid_base[2], spline[2], full_z, True)
    slope_z = spline_rows(grid_base[2], spline_slope[2], full_z, True)
    lifted = (rows_x[:, :, None] * rows_y[:, None, :]).reshape(atom_count, slab_width * full_y)
    lifted = jnp.concatenate([charge_a[:, None] * lifted, charge_b[:, None] * lifted], axis=1)
    spread = jnp.einsum("ar,az->rz", lifted, rows_z, precision=highest).reshape(
        2, slab_width, full_y, full_z
    )
    owned_grid = spread[:, :planes]
    for distance in range(1, hop_count + 1):
        first_layer = (distance - 1) * planes
        last_layer = min(distance * planes, margin)
        arrived = from_behind(spread[:, planes + first_layer : planes + last_layer], "px", distance)
        owned_grid = owned_grid.at[:, : last_layer - first_layer].add(arrived)
    real_part, imag_part = transform(owned_grid[0:1], owned_grid[1:2], 3, True)
    real_part, imag_part = transform(real_part, imag_part, 2, True)
    channels = real_part.shape[0]
    stacked = jnp.concatenate([real_part, imag_part], axis=0)
    columns = lax.all_to_all(stacked, "px", split_axis=2, concat_axis=1, tiled=True)
    real_part, imag_part = transform(columns[:channels], columns[channels:], 1, True)
    real_part = real_part * influence[None]
    imag_part = imag_part * influence[None]
    real_part, imag_part = transform(real_part, imag_part, 1, False)
    stacked = jnp.concatenate([real_part, imag_part], axis=0)
    returned = lax.all_to_all(stacked, "px", split_axis=1, concat_axis=2, tiled=True)
    real_part, imag_part = transform(returned[:channels], returned[channels:], 2, False)
    inverse_scale = 1.0 / (full_x * full_y * full_z)
    real_part, imag_part = transform(real_part, imag_part, 3, False)
    potential = jnp.concatenate([real_part, imag_part], axis=0) * inverse_scale
    pieces = [potential]
    for distance in range(1, hop_count + 1):
        first_layer = (distance - 1) * planes
        last_layer = min(distance * planes, margin)
        pieces.append(from_behind(potential, "px", -distance))
    potential = jnp.concatenate(pieces, axis=1)
    stacked_z = jnp.concatenate([rows_z, slope_z], axis=0)
    sampled = jnp.einsum(
        "az,rz->ar",
        stacked_z,
        potential.reshape(2 * slab_width * full_y, full_z),
        precision=highest,
    )
    sampled = sampled.reshape(2, atom_count, 2, slab_width, full_y)
    plain_z = sampled[0]
    slope_zed = sampled[1]
    along_y = jnp.einsum("aspy,ay->asp", plain_z, rows_y, precision=highest)
    slope_along_y = jnp.einsum("aspy,ay->asp", plain_z, slope_y, precision=highest)
    zed_along_y = jnp.einsum("aspy,ay->asp", slope_zed, rows_y, precision=highest)
    grad_x = jnp.einsum("asp,ap->sa", along_y, slope_x, precision=highest)
    grad_y = jnp.einsum("asp,ap->sa", slope_along_y, rows_x, precision=highest)
    grad_z = jnp.einsum("asp,ap->sa", zed_along_y, rows_x, precision=highest)
    gradient = jnp.stack([grad_x, grad_y, grad_z])
    reciprocal = -(
        (1.0 - weight_b) * charge_a * gradient[:, 0] + weight_b * charge_b * gradient[:, 1]
    )
    packet = jnp.concatenate([positions, charge_a[None], charge_b[None]], axis=0)
    to_right = jnp.take(packet, ghost_lists[0], axis=1)
    to_left = jnp.take(packet, ghost_lists[1], axis=1)
    from_left = from_behind(to_right, "px", 1)
    from_right = from_behind(to_left, "px", -1)
    from_left = from_left.at[0].add(jnp.where(me_index == 0, -float(full_x), 0.0))
    from_right = from_right.at[0].add(jnp.where(me_index == group_size - 1, float(full_x), 0.0))
    candidates = jnp.concatenate([packet, from_left, from_right], axis=1)
    real_space = device_pairs(packet, candidates, pair_tiles, weight_b)
    return reciprocal + real_space


def solution(mesh):
    placed = (
        P(("win", "px")),
        P(("win", "px")),
        P("win"),
        P(None, ("win", "px")),
        P(None, ("win", "px")),
        P(None, None, ("win", "px")),
        P(None, None, ("win", "px")),
        P(None, "px", None),
        P(("win", "px"), None),
        P(None, ("win", "px")),
    )
    return jax.shard_map(
        per_device, mesh=mesh, in_specs=placed, out_specs=P(None, ("win", "px")), check_vma=False
    )
```

profile of v0, /device:TPU:33, one launch (start us, length us, event | category | flops | bytes accessed | tf_op | source)
XLA Modules:
  0.0 403.5 jit_solution(11331851521763481988)
XLA Ops:
  1.4 2.2 fusion.202
  6.9 7.9 %select_add_fusion.1 = (f32[4096,128]{1,0:T(8,128)}, f32[4096,128]{1,0:T(8,128)S(1)}) fusion(f32[4096]{0:T(1024)S(1)} %bitcast.247, f32[4096]{0:T(1024)S(1)} %bitcast.248, f32[4096]{0:T(1024)S(1)} %bitcast.245, f32[4096]{0:T(1024)S(1)} %bitcast.246, s32[4096]{0:T(1024)S(1)} %get-tuple-element.300, s32[4096]{0:T(1024)S(1)} %get-tuple-element.299, ...), kind=kLoop, calls=%fused_computation.53 | loop fusion | flops 9437184 | bytes 4390912 | tf_op jit(solution)/shard_map/add | solution.py:56
  14.7 15.5 %broadcast_multiply_fusion = f32[4096,4,128]{2,1,0:T(4,128)S(1)} fusion(f32[4096,128]{1,0:T(8,128)S(1)} %get-tuple-element.284, f32[4096,4]{1,0:T(8,128)S(1)} %copy-done.3), kind=kLoop, calls=%fused_computation.52 | loop fusion | flops 2097152 | bytes 10551296 | tf_op jit(solution)/shard_map/mul | solution.py:118
  30.3 5.1 %bitcast_multiply_fusion.1 = (f32[4096,512]{1,0:T(8,128)S(1)}, f32[4096,512]{1,0:T(8,128)}) fusion(f32[512,8,4,128]{3,2,1,0:T(4,128)S(1)} %bitcast.209, f32[4096]{0:T(1024)S(1)} %copy-done.7, f32[4096]{0:T(1024)S(1)} %copy-done.6), kind=kLoop, calls=%fused_computation.47 | loop fusion | flops 4194304 | bytes 25198592 | tf_op jit(solution)/shard_map/mul | solution.py:119
  35.4 4.5 %select_add_fusion.11 = f32[4096,128]{1,0:T(8,128)S(1)} fusion(f32[4096]{0:T(1024)S(1)} %bitcast.226, s32[4096]{0:T(1024)S(1)} %get-tuple-element.293, f32[4096]{0:T(1024)S(1)} %bitcast.228, s32[4096]{0:T(1024)S(1)} %get-tuple-element.292, f32[4096]{0:T(1024)S(1)} %bitcast.230, s32[4096]{0:T(1024)S(1)} %get-tuple-element.291, ...), kind=kLoop, calls=%fused_computation.60.clone.clone.2 | loop fusion | flops 5767168 | bytes 2228224 | tf_op jit(solution)/shard_map/ar,az->rz/dot_general | solution.py:120
  39.9 27.4 %fusion.16 = f32[1024,128]{1,0:T(8,128)S(1)} fusion(f32[4096,512]{1,0:T(8,128)} %get-tuple-element.249, f32[4096,512]{1,0:T(8,128)S(1)} %get-tuple-element.248, f32[4096,128]{1,0:T(8,128)S(1)} %select_add_fusion.11), kind=kOutput, calls=%fused_computation.39 | convolution fusion | flops 6446645248 | bytes 19398656 | tf_op jit(solution)/shard_map/ar,az->rz/dot_general | solution.py:120
  68.1 3.8 collective-permute-start
  71.9 2.5 collective-permute-start.1
  74.4 2.5 collective-permute-start.2
  79.0 2.6 gather_fusion.1
  81.7 4.1 %collective-permute-start.6 = (f32[5,512]{0,1:T(8,128)S(1)}, f32[5,512]{0,1:T(8,128)S(1)}, u32[]{:S(2)}, u32[]{:S(2)}) collective-permute-start(f32[5,512]{0,1:T(8,128)S(1)} %select_bitcast_fusion.2), channel_id=1, source_target_pairs={{0,1},{1,2},{2,3},{3,4},{4,5},{5,6},{6,7},{7,8},{8,9},{9,10},{10,1... | collective-permute-start | bytes 30728 | tf_op jit(solution)/shard_map/ppermute | solution.py:19
  85.9 2.6 gather_fusion.2
  89.4 7.8 %collective-permute-start.7 = (f32[5,512]{0,1:T(8,128)}, f32[5,512]{0,1:T(8,128)S(1)}, u32[]{:S(2)}, u32[]{:S(2)}) collective-permute-start(f32[5,512]{0,1:T(8,128)} %select_bitcast_fusion.1), channel_id=1, source_target_pairs={{0,127},{1,0},{2,1},{3,2},{4,3},{5,4},{6,5},{7,6},{8,7},{9,8},{10,... | collective-permute-start | bytes 30728 | tf_op jit(solution)/shard_map/ppermute | solution.py:19
  97.2 2.5 collective-permute-done.1
  106.9 13.7 %all-to-all-start = ((f32[2,1,128,128]{3,1,0,2:T(1,128)}), f32[2,1,128,128]{3,1,0,2:T(1,128)S(1)}, u32[]{:S(2)}, u32[]{:S(2)}) async-start(f32[2,1,128,128]{3,1,0,2:T(1,128)} %copy.58), calls=%async_computation | async-start | bytes 262144 | tf_op jit(solution)/shard_map/all_to_all | solution.py:133
  120.7 9.8 %select_add_fusion.4 = (f32[4096,128]{1,0:T(8,128)}, f32[4096,128]{1,0:T(8,128)}) fusion(f32[4096]{0:T(1024)S(1)} %bitcast.227, s32[4096]{0:T(1024)S(1)} %copy-done.13, f32[4096]{0:T(1024)S(1)} %bitcast.229, s32[4096]{0:T(1024)S(1)} %copy-done.11, f32[4096]{0:T(1024)S(1)} %bitcast.231, s32[4096]{0:T(1024)S(1)} %copy-done.9, f32[4096]{0:T(1024)S(1)} %bitcast.225, ...), kind=kLoop, calls=%fused_computation.60 | loop fusion | flops 9437184 | bytes 4390912 | tf_op jit(solution)/shard_map/add | solution.py:56
  132.4 2.9 copy.102
  142.1 17.7 %all-to-all-start.1 = ((f32[2,128,1,128]{3,2,0,1:T(1,128)}), f32[2,128,1,128]{3,2,0,1:T(1,128)S(1)}, u32[]{:S(2)}, u32[]{:S(2)}) async-start(f32[2,128,1,128]{3,2,0,1:T(1,128)} %copy.60), calls=%async_computation.1 | async-start | bytes 262144 | tf_op jit(solution)/shard_map/all_to_all | solution.py:139
  162.0 14.5 %all-to-all-done.1 = f32[2,128,1,128]{3,2,0,1:T(1,128)S(1)} async-done(((f32[2,128,1,128]{3,2,0,1:T(1,128)}), f32[2,128,1,128]{3,2,0,1:T(1,128)S(1)}, u32[]{:S(2)}, u32[]{:S(2)}) %all-to-all-start.1) | async-done | bytes 131104 | tf_op jit(solution)/shard_map/all_to_all | solution.py:139
  183.4 175.8 %while.20 = (s32[]{:T(128)}, f32[3,32,128]{2,1,0:T(8,128)S(1)}, f32[]{:T(128)}, f32[5,32,128]{2,1,0:T(8,128)S(1)}, s32[12,32]{1,0:T(8,128)}, /*index=5*/f32[5,40...) while((s32[]{:T(128)}, f32[3,32,128]{2,1,0:T(8,128)S(1)}, f32[]{:T(128)}, ...), condition=%wide.region_3.5_spmd.clone, body=%wide.region_0.4_spmd.clone.sunk | while | flops 46179616 | bytes 9605943 | solution.py:85
  185.7 2.1 fusion.239
  188.4 5.8 %fusion.241 = f32[32,128,128]{2,1,0:T(8,128)S(1)} fusion(f32[32,128,128]{2,1,0:T(8,128)S(1)} %fusion.239, f32[32,128]{1,0:T(8,128)S(1)} %bitcast.213, f32[32,128]{1,0:T(8,128)S(1)} %get-tuple-element.354, f32[32,128]{1,0:T(8,128)S(1)} %bitcast.212, f32[32,128]{1,0:T(8,128)S(1)} %get-tuple-element.356), kind=kLoop, calls=%fused_computation.12.clone.1 | loop fusion | flops 37224448 | bytes 4259840 | tf_op jit(solution)/shard_map/while/body/eval_jaxpr/mul | solution.py:73
  194.3 3.8 fusion.242
  200.3 2.1 fusion.239
  203.1 5.8 %fusion.241 = f32[32,128,128]{2,1,0:T(8,128)S(1)} fusion(f32[32,128,128]{2,1,0:T(8,128)S(1)} %fusion.239, f32[32,128]{1,0:T(8,128)S(1)} %bitcast.213, f32[32,128]{1,0:T(8,128)S(1)} %get-tuple-element.354, f32[32,128]{1,0:T(8,128)S(1)} %bitcast.212, f32[32,128]{1,0:T(8,128)S(1)} %get-tuple-element.356), kind=kLoop, calls=%fused_computation.12.clone.1 | loop fusion | flops 37224448 | bytes 4259840 | tf_op jit(solution)/shard_map/while/body/eval_jaxpr/mul | solution.py:73
  208.9 3.8 fusion.242
  217.7 5.8 %fusion.241 = f32[32,128,128]{2,1,0:T(8,128)S(1)} fusion(f32[32,128,128]{2,1,0:T(8,128)S(1)} %fusion.239, f32[32,128]{1,0:T(8,128)S(1)} %bitcast.213, f32[32,128]{1,0:T(8,128)S(1)} %get-tuple-element.354, f32[32,128]{1,0:T(8,128)S(1)} %bitcast.212, f32[32,128]{1,0:T(8,128)S(1)} %get-tuple-element.356), kind=kLoop, calls=%fused_computation.12.clone.1 | loop fusion | flops 37224448 | bytes 4259840 | tf_op jit(solution)/shard_map/while/body/eval_jaxpr/mul | solution.py:73
  223.6 3.8 fusion.242
  232.4 5.8 %fusion.241 = f32[32,128,128]{2,1,0:T(8,128)S(1)} fusion(f32[32,128,128]{2,1,0:T(8,128)S(1)} %fusion.239, f32[32,128]{1,0:T(8,128)S(1)} %bitcast.213, f32[32,128]{1,0:T(8,128)S(1)} %get-tuple-element.354, f32[32,128]{1,0:T(8,128)S(1)} %bitcast.212, f32[32,128]{1,0:T(8,128)S(1)} %get-tuple-element.356), kind=kLoop, calls=%fused_computation.12.clone.1 | loop fusion | flops 37224448 | bytes 4259840 | tf_op jit(solution)/shard_map/while/body/eval_jaxpr/mul | solution.py:73
  238.2 3.8 fusion.242
  247.0 5.8 %fusion.241 = f32[32,128,128]{2,1,0:T(8,128)S(1)} fusion(f32[32,128,128]{2,1,0:T(8,128)S(1)} %fusion.239, f32[32,128]{1,0:T(8,128)S(1)} %bitcast.213, f32[32,128]{1,0:T(8,128)S(1)} %get-tuple-element.354, f32[32,128]{1,0:T(8,128)S(1)} %bitcast.212, f32[32,128]{1,0:T(8,128)S(1)} %get-tuple-element.356), kind=kLoop, calls=%fused_computation.12.clone.1 | loop fusion | flops 37224448 | bytes 4259840 | tf_op jit(solution)/shard_map/while/body/eval_jaxpr/mul | solution.py:73
  252.9 3.8 fusion.242
  261.7 5.8 %fusion.241 = f32[32,128,128]{2,1,0:T(8,128)S(1)} fusion(f32[32,128,128]{2,1,0:T(8,128)S(1)} %fusion.239, f32[32,128]{1,0:T(8,128)S(1)} %bitcast.213, f32[32,128]{1,0:T(8,128)S(1)} %get-tuple-element.354, f32[32,128]{1,0:T(8,128)S(1)} %bitcast.212, f32[32,128]{1,0:T(8,128)S(1)} %get-tuple-element.356), kind=kLoop, calls=%fused_computation.12.clone.1 | loop fusion | flops 37224448 | bytes 4259840 | tf_op jit(solution)/shard_map/while/body/eval_jaxpr/mul | solution.py:73
  267.5 3.8 fusion.242
  276.3 5.8 %fusion.241 = f32[32,128,128]{2,1,0:T(8,128)S(1)} fusion(f32[32,128,128]{2,1,0:T(8,128)S(1)} %fusion.239, f32[32,128]{1,0:T(8,128)S(1)} %bitcast.213, f32[32,128]{1,0:T(8,128)S(1)} %get-tuple-element.354, f32[32,128]{1,0:T(8,128)S(1)} %bitcast.212, f32[32,128]{1,0:T(8,128)S(1)} %get-tuple-element.356), kind=kLoop, calls=%fused_computation.12.clone.1 | loop fusion | flops 37224448 | bytes 4259840 | tf_op jit(solution)/shard_map/while/body/eval_jaxpr/mul | solution.py:73
  282.1 3.8 fusion.242
  291.0 5.8 %fusion.241 = f32[32,128,128]{2,1,0:T(8,128)S(1)} fusion(f32[32,128,128]{2,1,0:T(8,128)S(1)} %fusion.239, f32[32,128]{1,0:T(8,128)S(1)} %bitcast.213, f32[32,128]{1,0:T(8,128)S(1)} %get-tuple-element.354, f32[32,128]{1,0:T(8,128)S(1)} %bitcast.212, f32[32,128]{1,0:T(8,128)S(1)} %get-tuple-element.356), kind=kLoop, calls=%fused_computation.12.clone.1 | loop fusion | flops 37224448 | bytes 4259840 | tf_op jit(solution)/shard_map/while/body/eval_jaxpr/mul | solution.py:73
  296.8 3.8 fusion.242
  305.6 5.8 %fusion.241 = f32[32,128,128]{2,1,0:T(8,128)S(1)} fusion(f32[32,128,128]{2,1,0:T(8,128)S(1)} %fusion.239, f32[32,128]{1,0:T(8,128)S(1)} %bitcast.213, f32[32,128]{1,0:T(8,128)S(1)} %get-tuple-element.354, f32[32,128]{1,0:T(8,128)S(1)} %bitcast.212, f32[32,128]{1,0:T(8,128)S(1)} %get-tuple-element.356), kind=kLoop, calls=%fused_computation.12.clone.1 | loop fusion | flops 37224448 | bytes 4259840 | tf_op jit(solution)/shard_map/while/body/eval_jaxpr/mul | solution.py:73
  311.4 3.8 fusion.242
  320.2 5.8 %fusion.241 = f32[32,128,128]{2,1,0:T(8,128)S(1)} fusion(f32[32,128,128]{2,1,0:T(8,128)S(1)} %fusion.239, f32[32,128]{1,0:T(8,128)S(1)} %bitcast.213, f32[32,128]{1,0:T(8,128)S(1)} %get-tuple-element.354, f32[32,128]{1,0:T(8,128)S(1)} %bitcast.212, f32[32,128]{1,0:T(8,128)S(1)} %get-tuple-element.356), kind=kLoop, calls=%fused_computation.12.clone.1 | loop fusion | flops 37224448 | bytes 4259840 | tf_op jit(solution)/shard_map/while/body/eval_jaxpr/mul | solution.py:73
  326.1 3.8 fusion.242
  334.9 5.8 %fusion.241 = f32[32,128,128]{2,1,0:T(8,128)S(1)} fusion(f32[32,128,128]{2,1,0:T(8,128)S(1)} %fusion.239, f32[32,128]{1,0:T(8,128)S(1)} %bitcast.213, f32[32,128]{1,0:T(8,128)S(1)} %get-tuple-element.354, f32[32,128]{1,0:T(8,128)S(1)} %bitcast.212, f32[32,128]{1,0:T(8,128)S(1)} %get-tuple-element.356), kind=kLoop, calls=%fused_computation.12.clone.1 | loop fusion | flops 37224448 | bytes 4259840 | tf_op jit(solution)/shard_map/while/body/eval_jaxpr/mul | solution.py:73
  340.7 3.8 fusion.242
  349.5 5.8 %fusion.241 = f32[32,128,128]{2,1,0:T(8,128)S(1)} fusion(f32[32,128,128]{2,1,0:T(8,128)S(1)} %fusion.239, f32[32,128]{1,0:T(8,128)S(1)} %bitcast.213, f32[32,128]{1,0:T(8,128)S(1)} %get-tuple-element.354, f32[32,128]{1,0:T(8,128)S(1)} %bitcast.212, f32[32,128]{1,0:T(8,128)S(1)} %get-tuple-element.356), kind=kLoop, calls=%fused_computation.12.clone.1 | loop fusion | flops 37224448 | bytes 4259840 | tf_op jit(solution)/shard_map/while/body/eval_jaxpr/mul | solution.py:73
  355.4 3.8 fusion.242
  359.3 30.4 %fusion.20 = f32[8192,1024]{0,1:T(8,128)} fusion(f32[1024,128]{1,0:T(8,128)S(1)} %bitcast.210, f32[4096,128]{1,0:T(8,128)} %get-tuple-element.286, f32[4096,128]{1,0:T(8,128)S(1)} %copy-done), kind=kOutput, calls=%fused_computation.48 | convolution fusion | flops 12885950464 | bytes 38273024 | tf_op jit(solution)/shard_map/az,rz->ar/dot_general | solution.py:151
  389.7 12.4 %multiply_reduce_fusion.2 = (f32[4096,2,4]{0,2,1:T(4,128)S(1)}, f32[4096,2,4]{0,2,1:T(4,128)S(1)}, f32[4096,2,4]{0,2,1:T(4,128)S(1)}) fusion(f32[4096,128]{0,1:T(8,128)S(1)} %copy-done.1, f32[8192,1024]{0,1:T(8,128)} %fusion.20, f32[4096,128]{0,1:T(8,128)S(1)} %copy-done.2), kind=kLoop, calls=%fused_computation.45 | loop fusion | flops 25067520 | bytes 38141952 | tf_op jit(solution)/shard_map/aspy,ay->asp/dot_general | solution.py:160
  (262 shorter events, 88.4 us)
Async XLA Ops:
  6.8 28.5 %copy-start.8 = (s32[4096]{0:T(1024)}, s32[4096]{0:T(1024)S(1)}, u32[]{:S(2)}) copy-start(s32[4096]{0:T(1024)S(1)} %get-tuple-element.291) | copy-start | bytes 49156
  6.8 28.5 %copy-start.10 = (s32[4096]{0:T(1024)}, s32[4096]{0:T(1024)S(1)}, u32[]{:S(2)}) copy-start(s32[4096]{0:T(1024)S(1)} %get-tuple-element.292) | copy-start | bytes 49156
  6.8 28.5 %copy-start.12 = (s32[4096]{0:T(1024)}, s32[4096]{0:T(1024)S(1)}, u32[]{:S(2)}) copy-start(s32[4096]{0:T(1024)S(1)} %get-tuple-element.293) | copy-start | bytes 49156
  6.9 7.9 %copy-start.3 = (f32[4096,4]{1,0:T(8,128)S(1)}, f32[4096,4]{1,0:T(8,128)}, u32[]{:S(2)}) copy-start(f32[4096,4]{1,0:T(8,128)} %copy.57) | copy-start | bytes 196612
  14.7 15.5 %copy-start.6 = (f32[4096]{0:T(1024)S(1)}, f32[4096]{0:T(1024)}, u32[]{:S(2)}) copy-start(f32[4096]{0:T(1024)} %param.31) | copy-start | bytes 49156
  14.7 15.5 %copy-start.7 = (f32[4096]{0:T(1024)S(1)}, f32[4096]{0:T(1024)}, u32[]{:S(2)}) copy-start(f32[4096]{0:T(1024)} %param.30) | copy-start | bytes 49156
  39.9 37.0 %copy-start.18 = (s32[2,512]{1,0:T(2,128)S(1)}, s32[2,512]{1,0:T(2,128)}, u32[]{:S(2)}) copy-start(s32[2,512]{1,0:T(2,128)} %param.39) | copy-start | bytes 12292
  39.9 37.0 %copy-start.4 = (f32[3,4096]{1,0:T(4,128)S(1)}, f32[3,4096]{1,0:T(4,128)}, u32[]{:S(2)}) copy-start(f32[3,4096]{1,0:T(4,128)} %param.33) | copy-start | bytes 147460
  67.3 9.7 %copy-start.5 = (f32[1024,128]{1,0:T(8,128)}, f32[1024,128]{1,0:T(8,128)S(1)}, u32[]{:S(2)}) copy-start(f32[1024,128]{1,0:T(8,128)S(1)} %fusion.16) | copy-start | bytes 1572868
  68.1 29.1 %collective-permute-start = (f32[2,1,128,128]{3,2,1,0:T(8,128)}, f32[2,1,128,128]{3,2,1,0:T(8,128)}, u32[]{:S(2)}, u32[]{:S(2)}) collective-permute-start(f32[2,1,128,128]{3,2,1,0:T(8,128)} %get-tuple-element.250), channel_id=1, source_target_pairs={{0,1},{1,2},{2,3},{3,4},{4,5},{5,6},{6,7},{7,8},{8,9},{9,10},{10,1... | collective-permute-start | bytes 393224 | tf_op jit(solution)/shard_map/ppermute | solution.py:19
  71.9 27.8 %collective-permute-start.1 = (f32[2,1,128,128]{3,2,1,0:T(8,128)}, f32[2,1,128,128]{3,2,1,0:T(8,128)}, u32[]{:S(2)}, u32[]{:S(2)}) collective-permute-start(f32[2,1,128,128]{3,2,1,0:T(8,128)} %get-tuple-element.252), channel_id=1, source_target_pairs={{0,2},{1,3},{2,4},{3,5},{4,6},{5,7},{6,8},{7,9},{8,10},{9,11},{10,... | collective-permute-start | bytes 393224 | tf_op jit(solution)/shard_map/ppermute | solution.py:19
  74.4 26.9 %collective-permute-start.2 = (f32[2,1,128,128]{3,2,1,0:T(8,128)}, f32[2,1,128,128]{3,2,1,0:T(8,128)}, u32[]{:S(2)}, u32[]{:S(2)}) collective-permute-start(f32[2,1,128,128]{3,2,1,0:T(8,128)} %get-tuple-element.251), channel_id=1, source_target_pairs={{0,3},{1,4},{2,5},{3,6},{4,7},{5,8},{6,9},{7,10},{8,11},{9,12},{10... | collective-permute-start | bytes 393224 | tf_op jit(solution)/shard_map/ppermute | solution.py:19
  81.7 78.0 %collective-permute-start.6 = (f32[5,512]{0,1:T(8,128)S(1)}, f32[5,512]{0,1:T(8,128)S(1)}, u32[]{:S(2)}, u32[]{:S(2)}) collective-permute-start(f32[5,512]{0,1:T(8,128)S(1)} %select_bitcast_fusion.2), channel_id=1, source_target_pairs={{0,1},{1,2},{2,3},{3,4},{4,5},{5,6},{6,7},{7,8},{8,9},{9,10},{10,1... | collective-permute-start | bytes 30728 | tf_op jit(solution)/shard_map/ppermute | solution.py:19
  88.5 32.1 %copy-start.9 = (s32[4096]{0:T(1024)S(1)}, s32[4096]{0:T(1024)}, u32[]{:S(2)}) copy-start(s32[4096]{0:T(1024)} %copy-done.8) | copy-start | bytes 49156
  88.5 32.1 %copy-start.11 = (s32[4096]{0:T(1024)S(1)}, s32[4096]{0:T(1024)}, u32[]{:S(2)}) copy-start(s32[4096]{0:T(1024)} %copy-done.10) | copy-start | bytes 49156
  88.5 32.1 %copy-start.13 = (s32[4096]{0:T(1024)S(1)}, s32[4096]{0:T(1024)}, u32[]{:S(2)}) copy-start(s32[4096]{0:T(1024)} %copy-done.12) | copy-start | bytes 49156
  88.5 32.1 %copy-start.14 = (f32[1,1,4096]{2,1,0:T(1,128)S(1)}, f32[1,1,4096]{2,1,0:T(1,128)}, u32[]{:S(2)}) copy-start(f32[1,1,4096]{2,1,0:T(1,128)} %get-tuple-element.256) | copy-start | bytes 49156
  88.5 32.1 %copy-start.15 = (f32[1,1,4096]{2,1,0:T(1,128)S(1)}, f32[1,1,4096]{2,1,0:T(1,128)}, u32[]{:S(2)}) copy-start(f32[1,1,4096]{2,1,0:T(1,128)} %get-tuple-element.257) | copy-start | bytes 49156
  88.5 32.1 %copy-start.16 = (f32[1,1,4096]{2,1,0:T(1,128)S(1)}, f32[1,1,4096]{2,1,0:T(1,128)}, u32[]{:S(2)}) copy-start(f32[1,1,4096]{2,1,0:T(1,128)} %get-tuple-element.258) | copy-start | bytes 49156
  89.4 71.4 %collective-permute-start.7 = (f32[5,512]{0,1:T(8,128)}, f32[5,512]{0,1:T(8,128)S(1)}, u32[]{:S(2)}, u32[]{:S(2)}) collective-permute-start(f32[5,512]{0,1:T(8,128)} %select_bitcast_fusion.1), channel_id=1, source_target_pairs={{0,127},{1,0},{2,1},{3,2},{4,3},{5,4},{6,5},{7,6},{8,7},{9,8},{10,... | collective-permute-start | bytes 30728 | tf_op jit(solution)/shard_map/ppermute | solution.py:19
  106.9 30.7 %all-to-all-start = ((f32[2,1,128,128]{3,1,0,2:T(1,128)}), f32[2,1,128,128]{3,1,0,2:T(1,128)S(1)}, u32[]{:S(2)}, u32[]{:S(2)}) async-start(f32[2,1,128,128]{3,1,0,2:T(1,128)} %copy.58), calls=%async_computation | async-start | bytes 262144 | tf_op jit(solution)/shard_map/all_to_all | solution.py:133
  130.4 1.9 copy-start.17
  142.1 34.4 %all-to-all-start.1 = ((f32[2,128,1,128]{3,2,0,1:T(1,128)}), f32[2,128,1,128]{3,2,0,1:T(1,128)S(1)}, u32[]{:S(2)}, u32[]{:S(2)}) async-start(f32[2,128,1,128]{3,2,0,1:T(1,128)} %copy.60), calls=%async_computation.1 | async-start | bytes 262144 | tf_op jit(solution)/shard_map/all_to_all | solution.py:139
  180.3 178.9 %collective-permute-start.3 = (f32[2,1,128,128]{3,2,1,0:T(8,128)S(1)}, f32[2,1,128,128]{3,2,1,0:T(8,128)S(1)}, u32[]{:S(2)}, u32[]{:S(2)}) collective-permute-start(f32[2,1,128,128]{3,2,1,0:T(8,128)S(1)} %maximum_multiply_fusion), channel_id=1, source_target_pairs={{0,127},{1,0},{2,1},{3,2},{4,3},{5,4},{6,5},{7,6},{8,7},{9,8},{10,... | collective-permute-start | bytes 393224 | tf_op jit(solution)/shard_map/ppermute | solution.py:19
  182.3 176.9 %collective-permute-start.4 = (f32[2,1,128,128]{3,2,1,0:T(8,128)S(1)}, f32[2,1,128,128]{3,2,1,0:T(8,128)S(1)}, u32[]{:S(2)}, u32[]{:S(2)}) collective-permute-start(f32[2,1,128,128]{3,2,1,0:T(8,128)S(1)} %maximum_multiply_fusion), channel_id=1, source_target_pairs={{0,126},{1,127},{2,0},{3,1},{4,2},{5,3},{6,4},{7,5},{8,6},{9,7},{1... | collective-permute-start | bytes 393224 | tf_op jit(solution)/shard_map/ppermute | solution.py:19
  182.3 176.9 %collective-permute-start.5 = (f32[2,1,128,128]{3,2,1,0:T(8,128)S(1)}, f32[2,1,128,128]{3,2,1,0:T(8,128)S(1)}, u32[]{:S(2)}, u32[]{:S(2)}) collective-permute-start(f32[2,1,128,128]{3,2,1,0:T(8,128)S(1)} %maximum_multiply_fusion), channel_id=1, source_target_pairs={{0,125},{1,126},{2,127},{3,0},{4,1},{5,2},{6,3},{7,4},{8,5},{9,6},... | collective-permute-start | bytes 393224 | tf_op jit(solution)/shard_map/ppermute | solution.py:19
  183.4 175.9 %copy-start = (f32[4096,128]{1,0:T(8,128)S(1)}, f32[4096,128]{1,0:T(8,128)}, u32[]{:S(2)}) copy-start(f32[4096,128]{1,0:T(8,128)} %get-tuple-element.285) | copy-start | bytes 6291460
  359.3 30.4 %copy-start.1 = (f32[4096,128]{0,1:T(8,128)S(1)}, f32[4096,128]{0,1:T(8,128)}, u32[]{:S(2)}) copy-start(f32[4096,128]{0,1:T(8,128)} %copy.100) | copy-start | bytes 6291460
  359.3 30.4 %copy-start.2 = (f32[4096,128]{0,1:T(8,128)S(1)}, f32[4096,128]{0,1:T(8,128)}, u32[]{:S(2)}) copy-start(f32[4096,128]{0,1:T(8,128)} %copy.102) | copy-start | bytes 6291460
where the time goes:
time: 410 us; the launch traced here: 404 us
  other arithmetic  227 us (55%)
  matrix products  68.7 us (17%)
  starting transfers between devices  55.2 us (13%)
  local copies, waits for them, and re-layouts  30 us (7%)
  waiting for transfers between devices  20.1 us (5%)
    mul x12, other arithmetic, pair_block(): return jnp.sum((mixed * radial)[None] * separation, axis=3)  69.8 us
    reduce_sum x12, other arithmetic, pair_block(): return jnp.sum((mixed * radial)[None] * separation, axis=3)  46 us
    dot_general x1, matrix products, per_device(): jnp.einsum('az,rz->ar', stacked_z, potential.reshape(2 * slab_width * ful...  30.4 us
    dot_general x1, matrix products, per_device(): jnp.einsum('ar,az->rz', lifted, rows_z, precision=highest)  27.4 us
    reduce_sum x12, other arithmetic, pair_block(): dist_sq = jnp.sum(separation * separation, axis=0) + soften_sq  24.8 us
    ppermute x8, starting transfers between devices, from_behind(): return lax.ppermute(value, axis, pairs)  23.8 us
    add x3, other arithmetic, spline_rows(): result + jnp.where(target_cell[:, None] == cell_ids[None, :], weights[off...  17.8 us
    all_to_all x1, starting transfers between devices, per_device(): lax.all_to_all(stacked, 'px', split_axis=1, concat_axis=2, tiled=True)  17.7 us
  transfers between devices with their start and end apart: 10, of which 4 were waited for; matrix products, arithmetic and copies ran while one was open for 52% of the time, Pallas kernels for 0%

commit v1 on v0

v1 whole, which is shorter than its diff:
```python
import functools
import math
import numpy as np
import jax
import jax.numpy as jnp
from jax import lax
from jax.experimental import pallas as pl
from jax.experimental.pallas import tpu as pltpu
from jax.sharding import PartitionSpec as P

TILE = 128
beta = 0.35
soften_sq = 0.25
VMEM_LIMIT = 60 * 1024 * 1024


def low_part(value):
    return value - value.astype(jnp.bfloat16).astype(jnp.float32)


def three_parts(value):
    first = value.astype(jnp.bfloat16).astype(jnp.float32)
    rest = value - first
    second = rest.astype(jnp.bfloat16).astype(jnp.float32)
    return first, second, rest - second


def dot(left, right, dims=((1,), (0,))):
    return lax.dot_general(left, right, (dims, ((), ())), preferred_element_type=jnp.float32)


def dot3(left, right):
    return dot(left, right) + (dot(low_part(left), right) + dot(left, low_part(right)))


def spline_columns(base_row, weights, length):
    lanes = base_row.shape[1]
    cells = lax.broadcasted_iota(jnp.int32, (length, lanes), 0)
    offset = (cells - base_row) & (length - 1)
    results = []
    for table in weights:
        value = jnp.zeros((length, lanes), jnp.float32)
        for step in reversed(range(len(table))):
            value = jnp.where(offset == step, table[step], value)
        results.append(value)
    return results


def dft_tables(length):
    index = np.arange(length)
    angle = 2.0 * np.pi * ((index[:, None] * index[None, :]) % length) / length
    cosine, sine = np.cos(angle), np.sin(angle)
    forward = np.block([[cosine, -sine], [sine, cosine]]).astype(np.float32)
    return forward, np.ascontiguousarray(forward.T)


def spread_kernel(chunk, charges_ref, base_ref, spline_ref, packet_ref, ghost_ref,
                  *out_refs):
    layer_refs, left_ref, right_ref, total = out_refs[:-3], out_refs[-3], out_refs[-2], out_refs[-1]
    order = len(layer_refs)
    full_y, full_z = layer_refs[0].shape[1:]
    atoms = charges_ref.shape[1]
    ghosts = ghost_ref.shape[1]
    total[...] = jnp.zeros_like(total)

    def body(step, carry):
        at = pl.ds(pl.multiple_of(step * chunk, chunk), chunk)
        base = base_ref[:, at]
        weights = spline_ref[:, :, at]
        charges = charges_ref[:, at]
        rows_y, = spline_columns(base[1:2], [[weights[1, o][None] for o in range(order)]], full_y)
        rows_z, = spline_columns(base[2:3], [[weights[2, o][None] for o in range(order)]], full_z)
        both_z = jnp.concatenate([rows_z, low_part(rows_z)], axis=0)
        for state in range(2):
            for layer in range(order):
                row = charges[state:state + 1] * weights[0, layer][None]
                lifted = row * rows_y
                wide = dot(lifted, both_z, ((1,), (1,)))
                part = wide[:, :full_z] + wide[:, full_z:]
                part = part + dot(low_part(lifted), rows_z, ((1,), (1,)))
                at_rows = pl.ds((state * order + layer) * full_y, full_y)
                total[at_rows, :] += part
        return carry

    lax.fori_loop(0, atoms // chunk, body, 0)
    for state in range(2):
        for layer in range(order):
            first = (state * order + layer) * full_y
            layer_refs[layer][state] = total[first:first + full_y, :]

    def pick(step, carry):
        at = pl.ds(pl.multiple_of(step * chunk, chunk), chunk)
        rows = packet_ref[:, at]
        parts = jnp.concatenate(three_parts(rows), axis=0)
        ids = lax.broadcasted_iota(jnp.int32, (chunk, ghosts), 0) + step * chunk
        results = []
        for side in range(2):
            chosen = jnp.where(ids == ghost_ref[side:side + 1, :], 1.0, 0.0)
            results.append(carry[side] + dot(parts, chosen))
        return tuple(results)

    height = packet_ref.shape[0]
    start = jnp.zeros((3 * height, ghosts), jnp.float32)
    sides = lax.fori_loop(0, atoms // chunk, pick, (start, start))
    for ref, value in zip((left_ref, right_ref), sides):
        ref[...] = value[:height] + value[height:2 * height] + value[2 * height:]


def forward_kernel(own_ref, *refs):
    arrived, (table_ref, tablet_ref, out_ref) = refs[:-3], refs[-3:]
    full_y, full_z = own_ref.shape[1:]
    value = own_ref[...]
    for ref in arrived:
        value = value + ref[...]
    rows = jnp.concatenate([value[0], value[1]], axis=1)
    rows = dot3(rows, table_ref[...])
    columns = jnp.concatenate([rows[:, :full_z], rows[:, full_z:]], axis=0)
    columns = dot3(tablet_ref[...], columns)
    out_ref[0] = columns[:full_y]
    out_ref[1] = columns[full_y:]


def middle_kernel(scale, in_ref, influence_ref, table_ref, tablet_ref, out_ref):
    length = in_ref.shape[1]
    columns = jnp.concatenate([in_ref[0], in_ref[1]], axis=0)
    columns = dot3(tablet_ref[...], columns)
    gain = influence_ref[...] * scale
    columns = columns * jnp.concatenate([gain, gain], axis=0)
    columns = dot3(table_ref[...], columns)
    out_ref[0] = columns[:length]
    out_ref[1] = columns[length:]


def inverse_kernel(in_ref, table_ref, tablet_ref, out_ref):
    full_y, full_z = in_ref.shape[1:]
    columns = jnp.concatenate([in_ref[0], in_ref[1]], axis=0)
    columns = dot3(table_ref[...], columns)
    rows = jnp.concatenate([columns[:full_y], columns[full_y:]], axis=1)
    rows = dot3(rows, tablet_ref[...])
    out_ref[0] = rows[:, :full_z]
    out_ref[1] = rows[:, full_z:]


def sum_tiles(value):
    rows, lanes = value.shape
    return jnp.sum(value.reshape(rows // 8, 8, lanes), axis=0)


def gather_kernel(chunk, order, coupling_ref, charges_ref, base_ref, spline_ref, slope_ref,
                  real_ref, *refs):
    plane_refs, (out_ref, planes) = refs[:-2], refs[-2:]
    full_y, full_z = plane_refs[0].shape[1:]
    atoms = charges_ref.shape[1]
    weight_b = coupling_ref[0]
    for state in range(2):
        for layer in range(order):
            first = (state * order + layer) * full_y
            value = plane_refs[layer][state]
            planes[first:first + full_y, :full_z] = value
            planes[first:first + full_y, full_z:] = low_part(value)

    def body(step, carry):
        at = pl.ds(pl.multiple_of(step * chunk, chunk), chunk)
        base = base_ref[:, at]
        weights = spline_ref[:, :, at]
        slopes = slope_ref[:, :, at]
        charges = charges_ref[:, at]

        def both(axis):
            return spline_columns(
                base[axis:axis + 1],
                [[table[axis, o][None] for o in range(order)] for table in (weights, slopes)],
                full_y)

        rows_y, slope_y = both(1)
        rows_z, slope_z = both(2)
        stacked_z = jnp.concatenate([rows_z, slope_z], axis=1)
        twice_z = jnp.concatenate([stacked_z, stacked_z], axis=0)
        low_z = low_part(stacked_z)
        sums = [jnp.zeros((8, chunk), jnp.float32) for _ in range(3)]
        for state in range(2):
            mix = -(1.0 - weight_b) if state == 0 else -weight_b
            scale = charges[state:state + 1] * mix
            for layer in range(order):
                rows = planes[pl.ds((state * order + layer) * full_y, full_y), :]
                sampled = dot(rows, twice_z) + dot(rows[:, :full_z], low_z)
                plain, sloped = sampled[:, :chunk], sampled[:, chunk:]
                plain_x = scale * weights[0, layer][None]
                slope_x = scale * slopes[0, layer][None]
                sums[0] = sums[0] + slope_x * sum_tiles(plain * rows_y)
                sums[1] = sums[1] + plain_x * sum_tiles(plain * slope_y)
                sums[2] = sums[2] + plain_x * sum_tiles(sloped * rows_y)
        for axis in range(3):
            out_ref[axis:axis + 1, at] = (
                jnp.sum(sums[axis], axis=0, keepdims=True) + real_ref[axis:axis + 1, at])
        return carry

    lax.fori_loop(0, atoms // chunk, body, 0)


def pair_features(scaled, home):
    first, second, third = three_parts(scaled)
    square = jnp.sum(scaled * scaled, axis=0, keepdims=True)
    ones = jnp.ones_like(square)
    if home:
        square = three_parts(square + soften_sq * beta * beta)
        rows = [first, first, second, second, first, third, *square, ones, ones, ones]
    else:
        square = three_parts(square)
        rows = [-2.0 * part for part in (first, second, first, second, third, first)]
        rows = rows + [ones, ones, ones, *square]
    rows.append(jnp.zeros((8, scaled.shape[1]), jnp.float32))
    return jnp.concatenate(rows, axis=0)


def pair_place(rows, shift, first_tile, near_table, source_table, home_table):
    local = jnp.concatenate([rows[0:1] + (shift - 0.5), rows[1:3] - 4.0], axis=0)
    scaled = local * beta
    q_a, q_b = rows[3:4], rows[4:5]
    source = jnp.concatenate([q_a, q_a * local, q_b, q_b * local], axis=0)
    source = jnp.concatenate([*three_parts(source), jnp.zeros_like(source)], axis=0)
    near = pair_features(scaled, False)
    near = jnp.concatenate([near, near, jnp.zeros((64, rows.shape[1]), jnp.float32)], axis=0)
    home = None if home_table is None else pair_features(scaled, True)
    for tile in range(rows.shape[1] // TILE):
        part = slice(tile * TILE, (tile + 1) * TILE)
        near_table[first_tile + tile] = near[:, part].T
        source_table[first_tile + tile] = source[:, part]
        if home is not None:
            home_table[first_tile + tile] = home[:, part]


def pair_own(slab_start, packet_ref, near_table, source_table, home_table, width=512):
    def own(step, carry):
        at = pl.ds(pl.multiple_of(step * width, width), width)
        pair_place(packet_ref[:, at], -slab_start, step * (width // TILE), near_table, source_table,
                   home_table)
        return carry

    lax.fori_loop(0, packet_ref.shape[1] // width, own, 0)


def pair_ghosts(slab_start, length, left_ref, right_ref, is_first, is_last, tiles, near_table,
                source_table):
    extra = left_ref.shape[1] // TILE
    pair_place(left_ref[...], -slab_start - is_first * length, tiles, near_table, source_table, None)
    pair_place(right_ref[...], -slab_start + is_last * length, tiles + extra, near_table,
               source_table, None)


def pair_tile(tile, packet_ref, slab_start, weight_b, lists_ref, near_table, source_table, home_table,
              out_ref):
    slots = lists_ref.shape[1]
    at = pl.ds(pl.multiple_of(tile * TILE, TILE), TILE)
    home = home_table[tile]
    blank = jnp.zeros_like(home)
    rest = jnp.zeros((TILE - 2 * home.shape[0], 2 * TILE), jnp.float32)
    wide_home = jnp.concatenate(
        [jnp.concatenate([home, blank], axis=1), jnp.concatenate([blank, home], axis=1), rest], axis=0)
    lane = lax.broadcasted_iota(jnp.int32, (TILE, TILE), 1)
    total = jnp.zeros((32, 2 * TILE), jnp.float32)
    for slot in range(0, slots, 2):
        one, two = lists_ref[tile, slot], lists_ref[tile, slot + 1]
        near = jnp.where(lane < 32, near_table[one], near_table[two])
        source = jnp.concatenate([source_table[one], source_table[two]], axis=1)
        square = dot(near, wide_home)
        inverse = lax.rsqrt(square)
        tail = (1.0 - lax.erf(square * inverse)) * inverse
        gauss = jnp.exp2(square * (-1.0 / math.log(2.0))) * (2.0 / math.sqrt(math.pi))
        radial = (tail + gauss) * (inverse * inverse)
        low = low_part(radial)
        both = jnp.concatenate(
            [jnp.concatenate([radial[:, :TILE], low[:, :TILE]], axis=1),
             jnp.concatenate([radial[:, TILE:], low[:, TILE:]], axis=1)], axis=0)
        total = total + dot(source, both)
    sums = total[:, :TILE] + total[:, TILE:]
    sums = sums[0:8] + sums[8:16] + sums[16:24]
    rows = packet_ref[:, at]
    local = jnp.concatenate([rows[0:1] - (slab_start + 0.5), rows[1:3] - 4.0], axis=0)
    scale = beta ** 3
    part_a = local * sums[0:1] - sums[1:4]
    part_b = local * sums[4:5] - sums[5:8]
    out_ref[:, at] = (
        ((1.0 - weight_b) * scale) * rows[3:4] * part_a + (weight_b * scale) * rows[4:5] * part_b)


def pair_kernel(length, coupling_ref, place_ref, lists_ref, packet_ref, left_ref, right_ref, out_ref,
                near_table, source_table, home_table):
    slab_start = place_ref[0]
    tiles = lists_ref.shape[0]
    pair_own(slab_start, packet_ref, near_table, source_table, home_table)
    pair_ghosts(slab_start, length, left_ref, right_ref, place_ref[1], place_ref[2], tiles,
                near_table, source_table)

    def body(tile, carry):
        pair_tile(tile, packet_ref, slab_start, coupling_ref[0], lists_ref, near_table, source_table,
                  home_table, out_ref)
        return carry

    lax.fori_loop(0, tiles, body, 0)


VM = pl.BlockSpec(memory_space=pltpu.VMEM)
SM = pl.BlockSpec(memory_space=pltpu.SMEM)
params = pltpu.CompilerParams(vmem_limit_bytes=VMEM_LIMIT)


def f32(*shape):
    return jax.ShapeDtypeStruct(shape, jnp.float32)


def run_spread(charges, grid_base, spline, packet, ghosts, full_y, full_z, chunk=512):
    order = spline.shape[1]
    gh = ghosts.shape[1]
    return pl.pallas_call(
        functools.partial(spread_kernel, chunk),
        out_shape=[f32(2, full_y, full_z)] * order + [f32(8, gh)] * 2,
        in_specs=[VM] * 5, out_specs=[VM] * (order + 2),
        scratch_shapes=[pltpu.VMEM((2 * order * full_y, full_z), jnp.float32)],
        compiler_params=params,
    )(charges, grid_base, spline, packet, ghosts)


def run_gather(coupling, charges, grid_base, spline, slope, real, planes, chunk=128):
    order = spline.shape[1]
    full_y, full_z = planes[0].shape[1:]
    return pl.pallas_call(
        functools.partial(gather_kernel, chunk, order),
        out_shape=f32(3, charges.shape[1]),
        in_specs=[SM] + [VM] * (5 + order), out_specs=VM,
        scratch_shapes=[pltpu.VMEM((2 * order * full_y, 2 * full_z), jnp.float32)],
        compiler_params=params,
    )(coupling, charges, grid_base, spline, slope, real, *planes)


def run_pairs(length, coupling, place, lists, packet, left, right):
    tiles = packet.shape[1] // TILE
    every = tiles + 2 * (left.shape[1] // TILE)
    return pl.pallas_call(
        functools.partial(pair_kernel, length),
        out_shape=f32(3, packet.shape[1]),
        in_specs=[SM] * 3 + [VM] * 3, out_specs=VM,
        scratch_shapes=[pltpu.VMEM((every, TILE, TILE), jnp.float32),
                        pltpu.VMEM((every, 32, TILE), jnp.float32),
                        pltpu.VMEM((tiles, 32, TILE), jnp.float32)],
        compiler_params=params,
    )(coupling, place, lists, packet, left, right)


def run_plain(kernel, out_shape, *operands):
    return pl.pallas_call(
        kernel, out_shape=out_shape, in_specs=[VM] * len(operands), out_specs=VM,
        compiler_params=params)(*operands)


def from_behind(value, axis, steps):
    count = lax.axis_size(axis)
    pairs = [(source, (source + steps) % count) for source in range(count)]
    return lax.ppermute(value, axis, pairs)


def per_device(charge_a, charge_b, coupling, positions, grid_base, spline, spline_slope, influence,
               pair_tiles, ghost_lists):
    group_size = lax.axis_size("px")
    me_index = lax.axis_index("px")
    full_x, slab_y, full_z = influence.shape
    full_y = slab_y * group_size
    order = spline.shape[1]
    charges = jnp.stack([charge_a, charge_b])
    packet = jnp.concatenate(
        [positions, charges, jnp.zeros((3, charges.shape[1]), jnp.float32)], axis=0)
    *layers, to_right, to_left = run_spread(
        charges, grid_base, spline, packet, ghost_lists, full_y, full_z)
    arrived = [from_behind(layers[d], "px", d) for d in range(1, order)]
    from_left = from_behind(to_right, "px", 1)
    from_right = from_behind(to_left, "px", -1)
    table, tablet = (jnp.asarray(value) for value in dft_tables(full_x))
    plane_shape = f32(2, full_y, full_z)
    plane = run_plain(forward_kernel, plane_shape, layers[0], *arrived, table, tablet)
    columns = lax.all_to_all(
        plane[:, None], "px", split_axis=2, concat_axis=1, tiled=True)[:, :, 0]
    columns = run_plain(
        functools.partial(middle_kernel, 1.0 / (full_x * full_y * full_z)), f32(2, full_x, full_z),
        columns, influence[:, 0], table, tablet)
    plane = lax.all_to_all(
        columns[:, :, None], "px", split_axis=1, concat_axis=2, tiled=True)[:, 0]
    plane = run_plain(inverse_kernel, plane_shape, plane, table, tablet)
    planes = [plane] + [from_behind(plane, "px", -d) for d in range(1, order)]
    place = jnp.stack([me_index, me_index == 0, me_index == group_size - 1]).astype(jnp.float32)
    real_space = run_pairs(
        float(full_x), coupling, place, pair_tiles, packet, from_left, from_right)
    return run_gather(coupling, charges, grid_base, spline, spline_slope, real_space, planes)


def solution(mesh):
    placed = (
        P(("win", "px")),
        P(("win", "px")),
        P("win"),
        P(None, ("win", "px")),
        P(None, ("win", "px")),
        P(None, None, ("win", "px")),
        P(None, None, ("win", "px")),
        P(None, "px", None),
        P(("win", "px"), None),
        P(None, ("win", "px")),
    )
    return jax.shard_map(
        per_device, mesh=mesh, in_specs=placed, out_specs=P(None, ("win", "px")), check_vma=False
    )
```

time: 410 us -> 173 us (0.42); the launches traced: 404 us -> 172 us
  other arithmetic: 227 us -> 3.64 us
  matrix products: 68.7 us -> 0 us
  Pallas kernels: 0 us -> 64.3 us
  blocking collectives: 0 us -> 53.1 us
  starting transfers between devices: 55.2 us -> 12.9 us
  local copies, waits for them, and re-layouts: 30 us -> 6.68 us
  waiting for transfers between devices: 20.1 us -> 30.9 us
    mul x28 -> x0, other arithmetic: 98.3 us -> none  [the longest x12 69.8 us: pair_block(): return jnp.sum((mixed * radial)[None] * separation, axis=3)]
    reduce_sum x24 -> x0, other arithmetic: 70.8 us -> none  [the longest x12 46 us: pair_block(): return jnp.sum((mixed * radial)[None] * separation, axis=3)]
    dot_general x26 -> x0, matrix products: 68.7 us -> none  [the longest x1 30.4 us: per_device(): jnp.einsum('az,rz->ar', stacked_z, potential.reshape(2 * slab_width * ful...]
    pallas_call x0 -> x6, Pallas kernels: none -> 64.3 us  [the longest x1 26.7 us: run_pairs(): pl.pallas_call(functools.partial(pair_kernel, length), out_shape=f32(3, p...]
    all_to_all x0 -> x2, blocking collectives: none -> 53.1 us  [the longest x1 27.7 us: per_device(): lax.all_to_all(plane[:, None], 'px', split_axis=2, concat_axis=1, tiled=T...]
    all_to_all x2 -> x0, starting transfers between devices: 31.4 us -> none  [the longest x1 17.7 us: per_device(): lax.all_to_all(stacked, 'px', split_axis=1, concat_axis=2, tiled=True)]
    ppermute x8, waiting for transfers between devices: 4.09 us -> 30.9 us  [from_behind(): return lax.ppermute(value, axis, pairs)]
    add x20 -> x0, other arithmetic: 19.8 us -> none  [the longest x3 17.8 us: spline_rows(): result + jnp.where(target_cell[:, None] == cell_ids[None, :], weights[off...]
  transfers between devices with their start and end apart: 10 -> 8, of which waited for: 4 -> 4; matrix products, arithmetic and copies ran while one was open for 52% -> 1% of each run, Pallas kernels for 0% -> 15%
where the time goes in v1:
time: 173 us; the launch traced here: 172 us
  Pallas kernels  64.3 us (37%)
  blocking collectives  53.1 us (31%)
  waiting for transfers between devices  30.9 us (18%)
  starting transfers between devices  12.9 us (7%)
  local copies, waits for them, and re-layouts  6.68 us (4%)
  other arithmetic  3.64 us (2%)
    ppermute x8, waiting for transfers between devices, from_behind(): return lax.ppermute(value, axis, pairs)  30.9 us
    all_to_all x1, blocking collectives, per_device(): lax.all_to_all(plane[:, None], 'px', split_axis=2, concat_axis=1, tiled=T...  27.7 us
    pallas_call x1, Pallas kernels, run_pairs(): pl.pallas_call(functools.partial(pair_kernel, length), out_shape=f32(3, p...  26.7 us
    all_to_all x1, blocking collectives, per_device(): lax.all_to_all(columns[:, :, None], 'px', split_axis=1, concat_axis=2, ti...  25.4 us
    pallas_call x1, Pallas kernels, run_gather(): pl.pallas_call(functools.partial(gather_kernel, chunk, order), out_shape=...  17.5 us
    ppermute x8, starting transfers between devices, from_behind(): return lax.ppermute(value, axis, pairs)  12.9 us
    pallas_call x1, Pallas kernels, run_spread(): pl.pallas_call(functools.partial(spread_kernel, chunk), out_shape=[f32(2,...  12.9 us
    pallas_call x3, Pallas kernels, run_plain(): pl.pallas_call(kernel, out_shape=out_shape, in_specs=[VM] * len(operands)...  7.23 us
  transfers between devices with their start and end apart: 8, of which 4 were waited for; matrix products, arithmetic and copies ran while one was open for 1% of the time, Pallas kernels for 15%

profile of v1, /device:TPU:33, one launch (start us, length us, event | category | flops | bytes accessed | tf_op | source)
XLA Modules:
  0.0 172.3 jit_solution(16735441675634345203)
XLA Ops:
  0.0 0.1 pad.3.clone
  0.1 0.0 copy-start.6
  0.1 1.4 pad_maximum_fusion.charges_ref
  1.5 0.0 copy-done.6
  1.5 0.0 copy-done.7
  1.5 1.6 maximum_maximum_fusion.packet_ref
  3.1 12.9 %shard_map.118 = (f32[2,128,128]{2,1,0:T(8,128)}, f32[2,128,128]{2,1,0:T(8,128)}, f32[2,128,128]{2,1,0:T(8,128)}, f32[2,128,128]{2,1,0:T(8,128)}, f32[8,512]{1,0:T(8,128)}, /*index=5*/f32[8,512]{1,0:T(8,128)}) custom-call(f32[2,4096]{1,0:T(2,128)} %pad_maximum_fusion.charges_ref, s32[3,4096]{1,0:T(4,128)} %base_ref.3, f32[3,4,4096]{2,1,0:T(4,128)} %spline_ref.3, ...), custom_call_target="tpu_custom_call" | custom-call | tf_op jit(solution)/shard_map/pallas_call | solution.py:315
  16.0 3.8 %collective-permute-start.2 = (f32[2,128,128]{2,1,0:T(8,128)}, f32[2,128,128]{2,1,0:T(8,128)S(1)}, u32[]{:S(2)}, u32[]{:S(2)}) collective-permute-start(f32[2,128,128]{2,1,0:T(8,128)} %get-tuple-element.14), channel_id=1, source_target_pairs={{0,1},{1,2},{2,3},{3,4},{4,5},{5,6},{6,7},{7,8},{8,9},{9,10},{10,1... | collective-permute-start | bytes 393224 | tf_op jit(solution)/shard_map/ppermute | solution.py:359
  19.8 2.5 %collective-permute-start.3 = (f32[2,128,128]{2,1,0:T(8,128)}, f32[2,128,128]{2,1,0:T(8,128)S(1)}, u32[]{:S(2)}, u32[]{:S(2)}) collective-permute-start(f32[2,128,128]{2,1,0:T(8,128)} %get-tuple-element.15), channel_id=1, source_target_pairs={{0,2},{1,3},{2,4},{3,5},{4,6},{5,7},{6,8},{7,9},{8,10},{9,11},{10,... | collective-permute-start | bytes 393224 | tf_op jit(solution)/shard_map/ppermute | solution.py:359
  22.3 2.6 %collective-permute-start.4 = (f32[2,128,128]{2,1,0:T(8,128)}, f32[2,128,128]{2,1,0:T(8,128)S(1)}, u32[]{:S(2)}, u32[]{:S(2)}) collective-permute-start(f32[2,128,128]{2,1,0:T(8,128)} %get-tuple-element.16), channel_id=1, source_target_pairs={{0,3},{1,4},{2,5},{3,6},{4,7},{5,8},{6,9},{7,10},{8,11},{9,12},{10... | collective-permute-start | bytes 393224 | tf_op jit(solution)/shard_map/ppermute | solution.py:359
  24.8 12.6 %collective-permute-done.2.refs_0_ = f32[2,128,128]{2,1,0:T(8,128)S(1)} collective-permute-done((f32[2,128,128]{2,1,0:T(8,128)}, f32[2,128,128]{2,1,0:T(8,128)S(1)}, u32[]{:S(2)}, u32[]{:S(2)}) %collective-permute-start.2) | collective-permute-done | bytes 131104 | tf_op jit(solution)/shard_map/ppermute | solution.py:359
  37.4 9.9 %collective-permute-done.3.refs_1_ = f32[2,128,128]{2,1,0:T(8,128)S(1)} collective-permute-done((f32[2,128,128]{2,1,0:T(8,128)}, f32[2,128,128]{2,1,0:T(8,128)S(1)}, u32[]{:S(2)}, u32[]{:S(2)}) %collective-permute-start.3) | collective-permute-done | bytes 131104 | tf_op jit(solution)/shard_map/ppermute | solution.py:359
  47.4 1.8 %collective-permute-done.4.refs_2_ = f32[2,128,128]{2,1,0:T(8,128)S(1)} collective-permute-done((f32[2,128,128]{2,1,0:T(8,128)}, f32[2,128,128]{2,1,0:T(8,128)S(1)}, u32[]{:S(2)}, u32[]{:S(2)}) %collective-permute-start.4) | collective-permute-done | bytes 131104 | tf_op jit(solution)/shard_map/ppermute | solution.py:359
  49.1 0.0 copy-done
  49.1 0.0 copy-done.1
  49.2 0.6 copy-done.2
  49.8 2.5 %shard_map.120 = f32[2,128,128]{2,1,0:T(8,128)} custom-call(f32[2,128,128]{2,1,0:T(8,128)} %get-tuple-element.13.own_ref, f32[2,128,128]{2,1,0:T(8,128)} %copy-done, f32[2,128,128]{2,1,0:T(8,128)} %copy-done.1, f32[2,128,128]{2,1,0:T(8,128)} %copy-done.2, f32[256,256]{1,0:T(8,128)} %constant.14.clone.refs_3_.table_ref, ...), custom_call_target="tpu_custom_call" | custom-call | tf_op jit(solution)/shard_map/pallas_call | solution.py:351
  52.3 1.0 copy.15
  53.3 27.7 %all_to_all.8 = f32[2,1,128,128]{3,0,1,2:T(2,128)S(1)} all-to-all(f32[2,1,128,128]{3,0,1,2:T(2,128)S(1)} %copy.15), channel_id=1, replica_groups=mesh['win'=2,'px'=128] {'px'}, dimensions={2} | all-to-all | bytes 262144 | tf_op jit(solution)/shard_map/all_to_all | solution.py:380
  81.0 0.7 copy.22
  81.7 2.4 %shard_map.121 = f32[2,128,128]{2,1,0:T(8,128)} custom-call(f32[2,128,128]{2,1,0:T(8,128)} %bitcast.16, f32[128,128]{1,0:T(8,128)} %bitcast.22, f32[256,256]{1,0:T(8,128)} %constant.14.clone.refs_3_.table_ref, f32[256,256]{1,0:T(8,128)} %constant.15.clone.refs_4_.tablet_ref), custom_call_target="tpu_custom_call" | custom-call | tf_op jit(solution)/shard_map/pallas_call | solution.py:351
  84.1 1.0 copy.17
  85.1 25.4 %all_to_all.9 = f32[2,128,1,128]{3,0,2,1:T(2,128)S(1)} all-to-all(f32[2,128,1,128]{3,0,2,1:T(2,128)S(1)} %copy.17), channel_id=1, replica_groups=mesh['win'=2,'px'=128] {'px'}, dimensions={1} | all-to-all | bytes 262144 | tf_op jit(solution)/shard_map/all_to_all | solution.py:385
  110.6 0.7 copy.21
  111.2 2.3 %shard_map.122.refs_0_ = f32[2,128,128]{2,1,0:T(8,128)} custom-call(f32[2,128,128]{2,1,0:T(8,128)} %bitcast.15, f32[256,256]{1,0:T(8,128)} %constant.14.clone.refs_3_.table_ref, f32[256,256]{1,0:T(8,128)} %constant.15.clone.refs_4_.tablet_ref), custom_call_target="tpu_custom_call" | custom-call | tf_op jit(solution)/shard_map/pallas_call | solution.py:351
  113.5 1.3 collective-permute-start.7
  114.8 1.0 collective-permute-start.6
  115.8 0.0 collective-permute-start.5
  115.8 0.0 copy-done.12
  115.8 1.7 collective-permute-start
  117.5 0.0 copy-done.11
  117.5 0.0 collective-permute-start.1
  117.5 0.7 add_convert_fusion.place_ref
  118.9 0.0 copy-done.10
  118.9 0.7 copy.14.lists_ref
  119.6 0.0 collective-permute-done.left_ref
  119.6 6.6 %collective-permute-done.1.right_ref = f32[8,512]{1,0:T(8,128)S(1)} collective-permute-done((f32[8,512]{1,0:T(8,128)S(1)}, f32[8,512]{1,0:T(8,128)S(1)}, u32[]{:S(2)}, u32[]{:S(2)}) %collective-permute-start.1) | collective-permute-done | bytes 16416 | tf_op jit(solution)/shard_map/ppermute | solution.py:359
  126.1 0.0 copy-done.8
  126.1 0.6 copy-done.9
  126.7 26.7 %shard_map.119.real_ref = f32[3,4096]{1,0:T(4,128)} custom-call(f32[1]{0:T(128)S(6)} %copy.23.coupling_ref, f32[3]{0:T(128)} %add_convert_fusion.place_ref, s32[32,12]{1,0:T(8,128)} %copy.14.lists_ref, f32[8,4096]{1,0:T(8,128)} %maximum_maximum_fusion.packet_ref, f32[8,512]{1,0:T(8,128)} %copy-done.8, f32[8,512]{1,0:T(8,128)} %copy-done.9), custom_call_target="tpu_custom_call" | custom-call | tf_op jit(solution)/shard_map/pallas_call | solution.py:339
  153.4 0.0 collective-permute-done.7.refs_3_
  153.4 0.0 collective-permute-done.6.refs_2_
  153.4 0.0 copy-start.4
  153.4 0.0 collective-permute-done.5.refs_1_
  153.5 0.6 copy-done.3
  154.1 0.1 copy-done.4
  154.1 0.6 copy-done.5
  154.8 17.5 %shard_map.123 = f32[3,4096]{1,0:T(4,128)} custom-call(f32[1]{0:T(128)S(6)} %copy.23.coupling_ref, f32[2,4096]{1,0:T(2,128)} %pad_maximum_fusion.charges_ref, s32[3,4096]{1,0:T(4,128)} %base_ref.3, f32[3,4,4096]{2,1,0:T(4,128)} %spline_ref.3, f32[3,4,4096]{2,1,0:T(4,128)} %slope_ref.1, f32[3,4096]{1,0:T(4,128)} %shard_map.119.real_ref, ...), custom_call_target="tpu_custom_call" | custom-call | tf_op jit(solution)/shard_map/pallas_call | solution.py:327
  (12 shorter events, 0.0 us)
Async XLA Ops:
  0.1 1.4 copy-start.6
  0.1 1.4 copy-start.7
  16.0 21.5 %collective-permute-start.2 = (f32[2,128,128]{2,1,0:T(8,128)}, f32[2,128,128]{2,1,0:T(8,128)S(1)}, u32[]{:S(2)}, u32[]{:S(2)}) collective-permute-start(f32[2,128,128]{2,1,0:T(8,128)} %get-tuple-element.14), channel_id=1, source_target_pairs={{0,1},{1,2},{2,3},{3,4},{4,5},{5,6},{6,7},{7,8},{8,9},{9,10},{10,1... | collective-permute-start | bytes 393224 | tf_op jit(solution)/shard_map/ppermute | solution.py:359
  19.8 27.6 %collective-permute-start.3 = (f32[2,128,128]{2,1,0:T(8,128)}, f32[2,128,128]{2,1,0:T(8,128)S(1)}, u32[]{:S(2)}, u32[]{:S(2)}) collective-permute-start(f32[2,128,128]{2,1,0:T(8,128)} %get-tuple-element.15), channel_id=1, source_target_pairs={{0,2},{1,3},{2,4},{3,5},{4,6},{5,7},{6,8},{7,9},{8,10},{9,11},{10,... | collective-permute-start | bytes 393224 | tf_op jit(solution)/shard_map/ppermute | solution.py:359
  22.3 26.9 %collective-permute-start.4 = (f32[2,128,128]{2,1,0:T(8,128)}, f32[2,128,128]{2,1,0:T(8,128)S(1)}, u32[]{:S(2)}, u32[]{:S(2)}) collective-permute-start(f32[2,128,128]{2,1,0:T(8,128)} %get-tuple-element.16), channel_id=1, source_target_pairs={{0,3},{1,4},{2,5},{3,6},{4,7},{5,8},{6,9},{7,10},{8,11},{9,12},{10... | collective-permute-start | bytes 393224 | tf_op jit(solution)/shard_map/ppermute | solution.py:359
  37.4 11.7 %copy-start = (f32[2,128,128]{2,1,0:T(8,128)}, f32[2,128,128]{2,1,0:T(8,128)S(1)}, u32[]{:S(2)}) copy-start(f32[2,128,128]{2,1,0:T(8,128)S(1)} %collective-permute-done.2.refs_0_) | copy-start | bytes 393220
  47.4 1.8 %copy-start.1 = (f32[2,128,128]{2,1,0:T(8,128)}, f32[2,128,128]{2,1,0:T(8,128)S(1)}, u32[]{:S(2)}) copy-start(f32[2,128,128]{2,1,0:T(8,128)S(1)} %collective-permute-done.3.refs_1_) | copy-start | bytes 393220
  49.1 0.6 copy-start.2
  111.2 4.6 %copy-start.12 = (f32[8,512]{1,0:T(8,128)S(1)}, f32[8,512]{1,0:T(8,128)}, u32[]{:S(2)}) copy-start(f32[8,512]{1,0:T(8,128)} %get-tuple-element.11) | copy-start | bytes 49156
  111.2 6.3 %copy-start.11 = (f32[8,512]{1,0:T(8,128)S(1)}, f32[8,512]{1,0:T(8,128)}, u32[]{:S(2)}) copy-start(f32[8,512]{1,0:T(8,128)} %get-tuple-element.12) | copy-start | bytes 49156
  113.5 39.9 %collective-permute-start.7 = (f32[2,128,128]{2,1,0:T(8,128)}, f32[2,128,128]{2,1,0:T(8,128)S(1)}, u32[]{:S(2)}, u32[]{:S(2)}) collective-permute-start(f32[2,128,128]{2,1,0:T(8,128)} %shard_map.122.refs_0_), channel_id=1, source_target_pairs={{0,125},{1,126},{2,127},{3,0},{4,1},{5,2},{6,3},{7,4},{8,5},{9,6},... | collective-permute-start | bytes 393224 | tf_op jit(solution)/shard_map/ppermute | solution.py:359
  114.8 38.6 %collective-permute-start.6 = (f32[2,128,128]{2,1,0:T(8,128)}, f32[2,128,128]{2,1,0:T(8,128)S(1)}, u32[]{:S(2)}, u32[]{:S(2)}) collective-permute-start(f32[2,128,128]{2,1,0:T(8,128)} %shard_map.122.refs_0_), channel_id=1, source_target_pairs={{0,126},{1,127},{2,0},{3,1},{4,2},{5,3},{6,4},{7,5},{8,6},{9,7},{1... | collective-permute-start | bytes 393224 | tf_op jit(solution)/shard_map/ppermute | solution.py:359
  115.8 37.7 %collective-permute-start.5 = (f32[2,128,128]{2,1,0:T(8,128)}, f32[2,128,128]{2,1,0:T(8,128)S(1)}, u32[]{:S(2)}, u32[]{:S(2)}) collective-permute-start(f32[2,128,128]{2,1,0:T(8,128)} %shard_map.122.refs_0_), channel_id=1, source_target_pairs={{0,127},{1,0},{2,1},{3,2},{4,3},{5,4},{6,5},{7,6},{8,7},{9,8},{10,... | collective-permute-start | bytes 393224 | tf_op jit(solution)/shard_map/ppermute | solution.py:359
  115.8 3.7 %collective-permute-start = (f32[8,512]{1,0:T(8,128)S(1)}, f32[8,512]{1,0:T(8,128)S(1)}, u32[]{:S(2)}, u32[]{:S(2)}) collective-permute-start(f32[8,512]{1,0:T(8,128)S(1)} %copy-done.12), channel_id=1, source_target_pairs={{0,1},{1,2},{2,3},{3,4},{4,5},{5,6},{6,7},{7,8},{8,9},{9,10},{10,1... | collective-permute-start | bytes 49160 | tf_op jit(solution)/shard_map/ppermute | solution.py:359
  117.5 8.6 %collective-permute-start.1 = (f32[8,512]{1,0:T(8,128)S(1)}, f32[8,512]{1,0:T(8,128)S(1)}, u32[]{:S(2)}, u32[]{:S(2)}) collective-permute-start(f32[8,512]{1,0:T(8,128)S(1)} %copy-done.11), channel_id=1, source_target_pairs={{0,127},{1,0},{2,1},{3,2},{4,3},{5,4},{6,5},{7,6},{8,7},{9,8},{10,... | collective-permute-start | bytes 49160 | tf_op jit(solution)/shard_map/ppermute | solution.py:359
  117.5 1.3 copy-start.10
  119.6 6.6 %copy-start.8 = (f32[8,512]{1,0:T(8,128)}, f32[8,512]{1,0:T(8,128)S(1)}, u32[]{:S(2)}) copy-start(f32[8,512]{1,0:T(8,128)S(1)} %collective-permute-done.left_ref) | copy-start | bytes 49156
  126.1 0.6 copy-start.9
  153.4 0.6 copy-start.3
  153.4 0.7 copy-start.4
  154.1 0.6 copy-start.5

commit v2 on v1

v2 whole, which is shorter than its diff:
```python
import functools
import math
import numpy as np
import jax
import jax.numpy as jnp
from jax import lax
from jax.experimental import pallas as pl
from jax.experimental.pallas import tpu as pltpu
from jax.sharding import PartitionSpec as P

TILE = 128
beta = 0.35
soften_sq = 0.25
VMEM_LIMIT = 60 * 1024 * 1024


def low_part(value):
    return value - value.astype(jnp.bfloat16).astype(jnp.float32)


def three_parts(value):
    first = value.astype(jnp.bfloat16).astype(jnp.float32)
    rest = value - first
    second = rest.astype(jnp.bfloat16).astype(jnp.float32)
    return first, second, rest - second


def dot(left, right, dims=((1,), (0,))):
    return lax.dot_general(left, right, (dims, ((), ())), preferred_element_type=jnp.float32)


def dot3(left, right):
    return dot(left, right) + (dot(low_part(left), right) + dot(left, low_part(right)))


def spline_columns(base_row, weights, length):
    lanes = base_row.shape[1]
    cells = lax.broadcasted_iota(jnp.int32, (length, lanes), 0)
    offset = (cells - base_row) & (length - 1)
    results = []
    for table in weights:
        value = jnp.zeros((length, lanes), jnp.float32)
        for step in reversed(range(len(table))):
            value = jnp.where(offset == step, table[step], value)
        results.append(value)
    return results


def dft_tables(length):
    index = np.arange(length)
    angle = 2.0 * np.pi * ((index[:, None] * index[None, :]) % length) / length
    cosine, sine = np.cos(angle), np.sin(angle)
    forward = np.block([[cosine, -sine], [sine, cosine]]).astype(np.float32)
    return forward, np.ascontiguousarray(forward.T)


def sum_tiles(value):
    rows, lanes = value.shape
    return jnp.sum(value.reshape(rows // 8, 8, lanes), axis=0)


def gather_kernel(chunk, order, coupling_ref, charges_ref, base_ref, spline_ref, slope_ref,
                  real_ref, plane_ref, out_ref, planes):
    full_y, full_z = plane_ref.shape[2:]
    atoms = charges_ref.shape[1]
    weight_b = coupling_ref[0]
    for state in range(2):
        for layer in range(order):
            first = (state * order + layer) * full_y
            value = plane_ref[layer, state]
            planes[first:first + full_y, :full_z] = value
            planes[first:first + full_y, full_z:] = low_part(value)

    def body(step, carry):
        at = pl.ds(pl.multiple_of(step * chunk, chunk), chunk)
        base = base_ref[:, at]
        weights = spline_ref[:, :, at]
        slopes = slope_ref[:, :, at]
        charges = charges_ref[:, at]

        def both(axis):
            return spline_columns(
                base[axis:axis + 1],
                [[table[axis, o][None] for o in range(order)] for table in (weights, slopes)],
                full_y)

        rows_y, slope_y = both(1)
        rows_z, slope_z = both(2)
        stacked_z = jnp.concatenate([rows_z, slope_z], axis=1)
        twice_z = jnp.concatenate([stacked_z, stacked_z], axis=0)
        low_z = low_part(stacked_z)
        sums = [jnp.zeros((8, chunk), jnp.float32) for _ in range(3)]
        for state in range(2):
            mix = -(1.0 - weight_b) if state == 0 else -weight_b
            scale = charges[state:state + 1] * mix
            for layer in range(order):
                rows = planes[pl.ds((state * order + layer) * full_y, full_y), :]
                sampled = dot(rows, twice_z) + dot(rows[:, :full_z], low_z)
                plain, sloped = sampled[:, :chunk], sampled[:, chunk:]
                plain_x = scale * weights[0, layer][None]
                slope_x = scale * slopes[0, layer][None]
                sums[0] = sums[0] + slope_x * sum_tiles(plain * rows_y)
                sums[1] = sums[1] + plain_x * sum_tiles(plain * slope_y)
                sums[2] = sums[2] + plain_x * sum_tiles(sloped * rows_y)
        for axis in range(3):
            out_ref[axis:axis + 1, at] = (
                jnp.sum(sums[axis], axis=0, keepdims=True) + real_ref[axis:axis + 1, at])
        return carry

    lax.fori_loop(0, atoms // chunk, body, 0)


def pair_features(scaled, home):
    first, second, third = three_parts(scaled)
    square = jnp.sum(scaled * scaled, axis=0, keepdims=True)
    ones = jnp.ones_like(square)
    if home:
        square = three_parts(square + soften_sq * beta * beta)
        rows = [first, first, second, second, first, third, *square, ones, ones, ones]
    else:
        square = three_parts(square)
        rows = [-2.0 * part for part in (first, second, first, second, third, first)]
        rows = rows + [ones, ones, ones, *square]
    rows.append(jnp.zeros((8, scaled.shape[1]), jnp.float32))
    return jnp.concatenate(rows, axis=0)


def pair_place(rows, shift, first_tile, near_table, source_table, home_table):
    local = jnp.concatenate([rows[0:1] + (shift - 0.5), rows[1:3] - 4.0], axis=0)
    scaled = local * beta
    q_a, q_b = rows[3:4], rows[4:5]
    source = jnp.concatenate([q_a, q_a * local, q_b, q_b * local], axis=0)
    source = jnp.concatenate([*three_parts(source), jnp.zeros_like(source)], axis=0)
    near = pair_features(scaled, False)
    near = jnp.concatenate([near, near, jnp.zeros((64, rows.shape[1]), jnp.float32)], axis=0)
    home = None if home_table is None else pair_features(scaled, True)
    for tile in range(rows.shape[1] // TILE):
        part = slice(tile * TILE, (tile + 1) * TILE)
        near_table[first_tile + tile] = near[:, part].T
        source_table[first_tile + tile] = source[:, part]
        if home is not None:
            home_table[first_tile + tile] = home[:, part]


def pair_own(slab_start, packet_ref, near_table, source_table, home_table, width=512):
    def own(step, carry):
        at = pl.ds(pl.multiple_of(step * width, width), width)
        pair_place(packet_ref[:, at], -slab_start, step * (width // TILE), near_table, source_table,
                   home_table)
        return carry

    lax.fori_loop(0, packet_ref.shape[1] // width, own, 0)


def pair_ghosts(slab_start, length, left_ref, right_ref, is_first, is_last, tiles, near_table,
                source_table):
    extra = left_ref.shape[1] // TILE
    pair_place(left_ref[...], -slab_start - is_first * length, tiles, near_table, source_table, None)
    pair_place(right_ref[...], -slab_start + is_last * length, tiles + extra, near_table,
               source_table, None)


def pair_tile(tile, packet_ref, slab_start, weight_b, lists_ref, near_table, source_table, home_table,
              out_ref):
    slots = lists_ref.shape[1]
    at = pl.ds(pl.multiple_of(tile * TILE, TILE), TILE)
    home = home_table[tile]
    blank = jnp.zeros_like(home)
    rest = jnp.zeros((TILE - 2 * home.shape[0], 2 * TILE), jnp.float32)
    wide_home = jnp.concatenate(
        [jnp.concatenate([home, blank], axis=1), jnp.concatenate([blank, home], axis=1), rest], axis=0)
    lane = lax.broadcasted_iota(jnp.int32, (TILE, TILE), 1)
    total = jnp.zeros((32, 2 * TILE), jnp.float32)
    for slot in range(0, slots, 2):
        one, two = lists_ref[tile, slot], lists_ref[tile, slot + 1]
        near = jnp.where(lane < 32, near_table[one], near_table[two])
        source = jnp.concatenate([source_table[one], source_table[two]], axis=1)
        square = dot(near, wide_home)
        inverse = lax.rsqrt(square)
        tail = (1.0 - lax.erf(square * inverse)) * inverse
        gauss = jnp.exp2(square * (-1.0 / math.log(2.0))) * (2.0 / math.sqrt(math.pi))
        radial = (tail + gauss) * (inverse * inverse)
        low = low_part(radial)
        both = jnp.concatenate(
            [jnp.concatenate([radial[:, :TILE], low[:, :TILE]], axis=1),
             jnp.concatenate([radial[:, TILE:], low[:, TILE:]], axis=1)], axis=0)
        total = total + dot(source, both)
    sums = total[:, :TILE] + total[:, TILE:]
    sums = sums[0:8] + sums[8:16] + sums[16:24]
    rows = packet_ref[:, at]
    local = jnp.concatenate([rows[0:1] - (slab_start + 0.5), rows[1:3] - 4.0], axis=0)
    scale = beta ** 3
    part_a = local * sums[0:1] - sums[1:4]
    part_b = local * sums[4:5] - sums[5:8]
    out_ref[:, at] = (
        ((1.0 - weight_b) * scale) * rows[3:4] * part_a + (weight_b * scale) * rows[4:5] * part_b)


VM = pl.BlockSpec(memory_space=pltpu.VMEM)
SM = pl.BlockSpec(memory_space=pltpu.SMEM)
params = pltpu.CompilerParams(vmem_limit_bytes=VMEM_LIMIT)


def f32(*shape):
    return jax.ShapeDtypeStruct(shape, jnp.float32)


def run_gather(coupling, charges, grid_base, spline, slope, real, planes, chunk=128):
    order = spline.shape[1]
    full_y, full_z = planes.shape[2:]
    return pl.pallas_call(
        functools.partial(gather_kernel, chunk, order),
        out_shape=f32(3, charges.shape[1]),
        in_specs=[SM] + [VM] * 6, out_specs=VM,
        scratch_shapes=[pltpu.VMEM((2 * order * full_y, 2 * full_z), jnp.float32)],
        compiler_params=params,
    )(coupling, charges, grid_base, spline, slope, real, planes)


MESH = pl.DeviceIdType.MESH


def spread_atoms(chunk, charges_ref, base_ref, spline_ref, spread_out):
    order, _, full_y, full_z = spread_out.shape
    spread_out[...] = jnp.zeros_like(spread_out)

    def body(step, carry):
        at = pl.ds(pl.multiple_of(step * chunk, chunk), chunk)
        base = base_ref[:, at]
        weights = spline_ref[:, :, at]
        charges = charges_ref[:, at]
        rows_y, = spline_columns(base[1:2], [[weights[1, o][None] for o in range(order)]], full_y)
        rows_z, = spline_columns(base[2:3], [[weights[2, o][None] for o in range(order)]], full_z)
        both_z = jnp.concatenate([rows_z, low_part(rows_z)], axis=0)
        for state in range(2):
            for layer in range(order):
                row = charges[state:state + 1] * weights[0, layer][None]
                lifted = row * rows_y
                wide = dot(lifted, both_z, ((1,), (1,)))
                part = wide[:, :full_z] + wide[:, full_z:]
                part = part + dot(low_part(lifted), rows_z, ((1,), (1,)))
                spread_out[layer, state] += part
        return carry

    lax.fori_loop(0, charges_ref.shape[1] // chunk, body, 0)


def pick_ghosts(chunk, packet_ref, ghost_ref, ghost_out):
    height, atoms = packet_ref.shape
    ghosts = ghost_ref.shape[1]

    def pick(step, carry):
        at = pl.ds(pl.multiple_of(step * chunk, chunk), chunk)
        parts = jnp.concatenate(three_parts(packet_ref[:, at]), axis=0)
        ids = lax.broadcasted_iota(jnp.int32, (chunk, ghosts), 0) + step * chunk
        results = []
        for side in range(2):
            chosen = jnp.where(ids == ghost_ref[side:side + 1, :], 1.0, 0.0)
            results.append(carry[side] + dot(parts, chosen))
        return tuple(results)

    start = jnp.zeros((3 * height, ghosts), jnp.float32)
    sides = lax.fori_loop(0, atoms // chunk, pick, (start, start))
    for side, value in enumerate(sides):
        ghost_out[side] = value[:height] + value[height:2 * height] + value[2 * height:]


def step_kernel(group, windows, scale, coupling_ref, lists_ref, charges_ref, base_ref, spline_ref,
                packet_ref, ghost_ref, influence_ref, table_ref, tablet_ref,
                plane_ref, real_ref,
                spread_out, halo_in, ghost_out, ghost_in, there_out, there_in, back_out, back_in,
                plane_in, near_table, source_table, home_table,
                halo_send, halo_recv, ghost_send, ghost_recv, row_send, row_recv, row_own,
                plane_send, plane_recv):
    me = lax.axis_index("px")
    order, _, full_y, full_z = spread_out.shape
    full_x = influence_ref.shape[0]
    tiles = lists_ref.shape[0]
    slab_start = me.astype(jnp.float32)

    def other(steps):
        return {"px": lax.rem(me + (steps + group), group)}

    barrier = pltpu.get_barrier_semaphore()

    def greet(steps, carry):
        pl.semaphore_signal(barrier, inc=1, device_id=other(steps), device_id_type=MESH)
        return carry

    lax.fori_loop(1, group, greet, 0)

    spread_atoms(512, charges_ref, base_ref, spline_ref, spread_out)
    pick_ghosts(512, packet_ref, ghost_ref, ghost_out)

    pl.semaphore_wait(barrier, group - 1)

    halos = [
        pltpu.make_async_remote_copy(
            src_ref=spread_out.at[layer], dst_ref=halo_in.at[layer - 1],
            send_sem=halo_send.at[layer - 1], recv_sem=halo_recv.at[layer - 1],
            device_id=other(layer), device_id_type=MESH)
        for layer in range(1, order)]
    visits = [
        pltpu.make_async_remote_copy(
            src_ref=ghost_out.at[side], dst_ref=ghost_in.at[side],
            send_sem=ghost_send.at[side], recv_sem=ghost_recv.at[side],
            device_id=other(1 - 2 * side), device_id_type=MESH)
        for side in range(2)]
    for copy in halos + visits:
        copy.start()
    pair_own(slab_start, packet_ref, near_table, source_table, home_table)
    for copy in halos + visits:
        copy.wait()

    def swap_rows(out_rows, in_rows, which):
        def row_to(steps):
            return pltpu.make_async_remote_copy(
                src_ref=out_rows.at[lax.rem(me + steps, group)], dst_ref=in_rows.at[me],
                send_sem=row_send.at[which], recv_sem=row_recv.at[which],
                device_id=other(steps), device_id_type=MESH)

        own = pltpu.make_async_copy(out_rows.at[me], in_rows.at[me], row_own.at[which])
        own.start()
        half = group // 2
        row_to(half).start()

        def send(steps, carry):
            row_to(half - steps).start()
            row_to(half + steps).start()
            return carry

        lax.fori_loop(1, half, send, 0)

        def finish():
            own.wait()
            every = pltpu.make_async_remote_copy(
                src_ref=out_rows.at[pl.ds(0, group - 1)], dst_ref=in_rows.at[pl.ds(0, group - 1)],
                send_sem=row_send.at[which], recv_sem=row_recv.at[which],
                device_id=other(half), device_id_type=MESH)
            every.wait()

        return finish

    def pairs(first, last):
        def body(tile, carry):
            pair_tile(tile, packet_ref, slab_start, coupling_ref[0], lists_ref, near_table,
                      source_table, home_table, real_ref)
            return carry

        lax.fori_loop(first, last, body, 0)

    table, tablet = table_ref[...], tablet_ref[...]
    value = spread_out[0]
    for layer in range(order - 1):
        value = value + halo_in[layer]
    rows = dot3(jnp.concatenate([value[0], value[1]], axis=1), table)
    columns = dot3(tablet, jnp.concatenate([rows[:, :full_z], rows[:, full_z:]], axis=0))
    there_out[:, 0, :] = columns[:full_y]
    there_out[:, 1, :] = columns[full_y:]
    finish = swap_rows(there_out, there_in, 0)

    is_first = jnp.where(me == 0, 1.0, 0.0)
    is_last = jnp.where(me == group - 1, 1.0, 0.0)
    pair_ghosts(slab_start, float(full_x), ghost_in.at[0], ghost_in.at[1], is_first, is_last, tiles,
                near_table, source_table)
    pairs(0, windows[0])
    finish()

    columns = dot3(tablet, jnp.concatenate([there_in[:, 0, :], there_in[:, 1, :]], axis=0))
    gain = influence_ref[...] * scale
    columns = dot3(table, columns * jnp.concatenate([gain, gain], axis=0))
    back_out[:, 0, :] = columns[:full_x]
    back_out[:, 1, :] = columns[full_x:]
    finish = swap_rows(back_out, back_in, 1)
    pairs(windows[0], windows[1])
    finish()

    columns = dot3(table, jnp.concatenate([back_in[:, 0, :], back_in[:, 1, :]], axis=0))
    rows = dot3(jnp.concatenate([columns[:full_y], columns[full_y:]], axis=1), tablet)
    plane_in[0, 0] = rows[:, :full_z]
    plane_in[0, 1] = rows[:, full_z:]
    lends = [
        pltpu.make_async_remote_copy(
            src_ref=plane_in.at[0], dst_ref=plane_in.at[layer],
            send_sem=plane_send.at[layer - 1], recv_sem=plane_recv.at[layer - 1],
            device_id=other(-layer), device_id_type=MESH)
        for layer in range(1, order)]
    for copy in lends:
        copy.start()
    pairs(windows[1], tiles)
    for copy in lends:
        copy.wait()
    plane_ref[...] = plane_in[...]


def run_step(group, coupling, lists, charges, grid_base, spline, packet, ghosts, influence):
    order = spline.shape[1]
    full_x, full_z = influence.shape
    full_y = group
    atoms = charges.shape[1]
    tiles = lists.shape[0]
    visitors = ghosts.shape[1]
    every = tiles + 2 * (visitors // TILE)
    plane = (2, full_y, full_z)
    table, tablet = (jnp.asarray(value) for value in dft_tables(full_x))
    windows = (tiles * 3 // 8, tiles * 6 // 8)
    return pl.pallas_call(
        functools.partial(step_kernel, group, windows, 1.0 / (full_x * full_y * full_z)),
        out_shape=[f32(order, *plane), f32(3, atoms)],
        in_specs=[SM] * 2 + [VM] * 8,
        out_specs=[VM] * 2,
        scratch_shapes=[
            pltpu.VMEM((order, *plane), jnp.float32),
            pltpu.VMEM((order - 1, *plane), jnp.float32),
            pltpu.VMEM((2, packet.shape[0], visitors), jnp.float32),
            pltpu.VMEM((2, packet.shape[0], visitors), jnp.float32),
            pltpu.VMEM((group, 2, full_z), jnp.float32),
            pltpu.VMEM((group, 2, full_z), jnp.float32),
            pltpu.VMEM((group, 2, full_z), jnp.float32),
            pltpu.VMEM((group, 2, full_z), jnp.float32),
            pltpu.VMEM((order, *plane), jnp.float32),
            pltpu.VMEM((every, TILE, TILE), jnp.float32),
            pltpu.VMEM((every, 32, TILE), jnp.float32),
            pltpu.VMEM((tiles, 32, TILE), jnp.float32),
            pltpu.SemaphoreType.DMA((order - 1,)),
            pltpu.SemaphoreType.DMA((order - 1,)),
            pltpu.SemaphoreType.DMA((2,)),
            pltpu.SemaphoreType.DMA((2,)),
            pltpu.SemaphoreType.DMA((2,)),
            pltpu.SemaphoreType.DMA((2,)),
            pltpu.SemaphoreType.DMA((2,)),
            pltpu.SemaphoreType.DMA((order - 1,)),
            pltpu.SemaphoreType.DMA((order - 1,)),
        ],
        compiler_params=pltpu.CompilerParams(
            vmem_limit_bytes=VMEM_LIMIT, collective_id=0, has_side_effects=True),
    )(coupling, lists, charges, grid_base, spline, packet, ghosts, influence, table, tablet)


def per_device(charge_a, charge_b, coupling, positions, grid_base, spline, spline_slope, influence,
               pair_tiles, ghost_lists):
    group = lax.axis_size("px")
    charges = jnp.stack([charge_a, charge_b])
    packet = jnp.concatenate(
        [positions, charges, jnp.zeros((3, charges.shape[1]), jnp.float32)], axis=0)
    planes, real_space = run_step(
        group, coupling, pair_tiles, charges, grid_base, spline, packet, ghost_lists, influence[:, 0])
    return run_gather(coupling, charges, grid_base, spline, spline_slope, real_space, planes)


def solution(mesh):
    placed = (
        P(("win", "px")),
        P(("win", "px")),
        P("win"),
        P(None, ("win", "px")),
        P(None, ("win", "px")),
        P(None, None, ("win", "px")),
        P(None, None, ("win", "px")),
        P(None, "px", None),
        P(("win", "px"), None),
        P(None, ("win", "px")),
    )
    return jax.shard_map(
        per_device, mesh=mesh, in_specs=placed, out_specs=P(None, ("win", "px")), check_vma=False
    )
```

time: 173 us -> 109 us (0.63)
  blocking collectives: 53.1 us -> 0 us
  Pallas kernels: 64.3 us -> 105 us
  waiting for transfers between devices: 30.9 us -> 0 us
  starting transfers between devices: 12.9 us -> 0 us
  local copies, waits for them, and re-layouts: 6.68 us -> 1.47 us
  other arithmetic: 3.64 us -> 1.35 us
    all_to_all x2 -> x0, blocking collectives: 53.1 us -> none  [the longest x1 27.7 us: per_device(): lax.all_to_all(plane[:, None], 'px', split_axis=2, concat_axis=1, tiled=T...]
    pallas_call x5 -> x1, Pallas kernels: 46.8 us -> 87.7 us  [run_step(): pl.pallas_call(functools.partial(step_kernel, group, windows, 1.0 / (full...]
    ppermute x8 -> x0, waiting for transfers between devices: 30.9 us -> none  [from_behind(): return lax.ppermute(value, axis, pairs)]
    ppermute x8 -> x0, starting transfers between devices: 12.9 us -> none  [from_behind(): return lax.ppermute(value, axis, pairs)]
    broadcast_in_dim x2 -> x0, local copies, waits for them, and re-layouts: 2.01 us -> none  [the longest x1 1.01 us: per_device(): plane[:, None]]
    unnamed x27 -> x7, local copies, waits for them, and re-layouts: 3.27 us -> 1.39 us
  transfers between devices with their start and end apart: 8 -> 0, of which waited for: 4 -> 0; matrix products, arithmetic and copies ran while one was open for 1% -> 0% of each run, Pallas kernels for 15% -> 0%
where the time goes in v2:
time: 109 us
  Pallas kernels  105 us (96%)
  local copies, waits for them, and re-layouts  1.47 us (1%)
  other arithmetic  1.35 us (1%)
    pallas_call x1, Pallas kernels, run_step(): pl.pallas_call(functools.partial(step_kernel, group, windows, 1.0 / (full...  87.7 us
    pallas_call x1, Pallas kernels, run_gather(): pl.pallas_call(functools.partial(gather_kernel, chunk, order), out_shape=...  17.5 us

profile of v2, /device:TPU:33, one launch (start us, length us, event | category | flops | bytes accessed | tf_op | source)
XLA Modules:
  0.0 108.8 jit_solution(2504600301422250881)
XLA Ops:
  0.7 0.0 copy-start.1
  0.7 0.0 copy-start
  0.7 0.0 copy-start.2
  0.7 0.1 pad.3.clone
  0.8 1.4 %copy.13.lists_ref = s32[32,12]{1,0:T(8,128)} copy(s32[32,12]{0,1:T(8,128)} %param.20) | data formatting | bytes 3072 | tf_op args[8]
  2.1 0.0 copy-done.1
  2.2 0.0 copy-done
  2.2 0.6 pad_maximum_fusion.charges_ref
  2.8 0.0 copy-done.2
  2.8 0.7 maximum_maximum_fusion.packet_ref
  3.5 87.7 %shard_map.118 = (f32[4,2,128,128]{3,2,1,0:T(8,128)}, f32[3,4096]{1,0:T(4,128)}) custom-call(f32[1]{0:T(128)S(6)} %copy.14.coupling_ref, s32[32,12]{1,0:T(8,128)} %copy.13.lists_ref, f32[2,4096]{1,0:T(2,128)} %pad_maximum_fusion.charges_ref, s32[3,4096]{1,0:T(4,128)} %base_ref.3, f32[3,4,4096]{2,1,0:T(4,128)} %spline_ref.3, ...), custom_call_target="tpu_custom_call" | custom-call | tf_op jit(solution)/shard_map/pallas_call | solution.py:407
  91.2 17.5 %shard_map.119 = f32[3,4096]{1,0:T(4,128)} custom-call(f32[1]{0:T(128)S(6)} %copy.14.coupling_ref, f32[2,4096]{1,0:T(2,128)} %pad_maximum_fusion.charges_ref, s32[3,4096]{1,0:T(4,128)} %base_ref.3, f32[3,4,4096]{2,1,0:T(4,128)} %spline_ref.3, f32[3,4,4096]{2,1,0:T(4,128)} %slope_ref.1, f32[3,4096]{1,0:T(4,128)} %get-tuple-element.7.real_ref, ...), custom_call_target="tpu_custom_call" | custom-call | tf_op jit(solution)/shard_map/pallas_call | solution.py:211
  (1 shorter events, 0.0 us)
Async XLA Ops:
  0.7 1.5 %copy-start.1 = (f32[4096]{0:T(1024)S(1)}, f32[4096]{0:T(1024)}, u32[]{:S(2)}) copy-start(f32[4096]{0:T(1024)} %param.12) | copy-start | bytes 49156
  0.7 1.5 %copy-start = (f32[4096]{0:T(1024)S(1)}, f32[4096]{0:T(1024)}, u32[]{:S(2)}) copy-start(f32[4096]{0:T(1024)} %param.13) | copy-start | bytes 49156
  0.7 2.1 %copy-start.2 = (f32[3,4096]{1,0:T(4,128)S(1)}, f32[3,4096]{1,0:T(4,128)}, u32[]{:S(2)}) copy-start(f32[3,4096]{1,0:T(4,128)} %param.15) | copy-start | bytes 147460

commit v3 on v2

v3 whole, which is shorter than its diff:
```python
import functools
import math
import numpy as np
import jax
import jax.numpy as jnp
from jax import lax
from jax.experimental import pallas as pl
from jax.experimental.pallas import tpu as pltpu
from jax.sharding import PartitionSpec as P

TILE = 128
beta = 0.35
soften_sq = 0.25
VMEM_LIMIT = 60 * 1024 * 1024


def low_part(value):
    return value - value.astype(jnp.bfloat16).astype(jnp.float32)


def three_parts(value):
    first = value.astype(jnp.bfloat16).astype(jnp.float32)
    rest = value - first
    second = rest.astype(jnp.bfloat16).astype(jnp.float32)
    return first, second, rest - second


def dot(left, right, dims=((1,), (0,))):
    return lax.dot_general(left, right, (dims, ((), ())), preferred_element_type=jnp.float32)


def dot3(left, right):
    return dot(left, right) + (dot(low_part(left), right) + dot(left, low_part(right)))


def spline_columns(base_row, weights, length):
    lanes = base_row.shape[1]
    cells = lax.broadcasted_iota(jnp.int32, (length, lanes), 0)
    offset = (cells - base_row) & (length - 1)
    results = []
    for table in weights:
        value = jnp.zeros((length, lanes), jnp.float32)
        for step in reversed(range(len(table))):
            value = jnp.where(offset == step, table[step], value)
        results.append(value)
    return results


def dft_tables(length):
    index = np.arange(length)
    angle = 2.0 * np.pi * ((index[:, None] * index[None, :]) % length) / length
    cosine, sine = np.cos(angle), np.sin(angle)
    forward = np.block([[cosine, -sine], [sine, cosine]]).astype(np.float32)
    return forward, np.ascontiguousarray(forward.T)


def sum_tiles(value):
    rows, lanes = value.shape
    return jnp.sum(value.reshape(rows // 8, 8, lanes), axis=0)


def pair_features(scaled, home):
    first, second, third = three_parts(scaled)
    square = jnp.sum(scaled * scaled, axis=0, keepdims=True)
    ones = jnp.ones_like(square)
    if home:
        square = three_parts(square + soften_sq * beta * beta)
        rows = [first, first, second, second, first, third, *square, ones, ones, ones]
    else:
        square = three_parts(square)
        rows = [-2.0 * part for part in (first, second, first, second, third, first)]
        rows = rows + [ones, ones, ones, *square]
    rows.append(jnp.zeros((8, scaled.shape[1]), jnp.float32))
    return jnp.concatenate(rows, axis=0)


def pair_place(rows, shift, first_tile, near_table, source_table, home_table):
    local = jnp.concatenate([rows[0:1] + (shift - 0.5), rows[1:3] - 4.0], axis=0)
    scaled = local * beta
    q_a, q_b = rows[3:4], rows[4:5]
    source = jnp.concatenate([q_a, q_a * local, q_b, q_b * local], axis=0)
    source = jnp.concatenate([*three_parts(source), jnp.zeros_like(source)], axis=0)
    near = pair_features(scaled, False)
    near = jnp.concatenate([near, near, jnp.zeros((64, rows.shape[1]), jnp.float32)], axis=0)
    home = None if home_table is None else pair_features(scaled, True)
    for tile in range(rows.shape[1] // TILE):
        part = slice(tile * TILE, (tile + 1) * TILE)
        near_table[first_tile + tile] = near[:, part].T
        source_table[first_tile + tile] = source[:, part]
        if home is not None:
            home_table[first_tile + tile] = home[:, part]


def pair_own(slab_start, packet_ref, near_table, source_table, home_table, width=512):
    def own(step, carry):
        at = pl.ds(pl.multiple_of(step * width, width), width)
        pair_place(packet_ref[:, at], -slab_start, step * (width // TILE), near_table, source_table,
                   home_table)
        return carry

    lax.fori_loop(0, packet_ref.shape[1] // width, own, 0)


def pair_ghosts(slab_start, length, left_ref, right_ref, is_first, is_last, tiles, near_table,
                source_table):
    extra = left_ref.shape[1] // TILE
    pair_place(left_ref[...], -slab_start - is_first * length, tiles, near_table, source_table, None)
    pair_place(right_ref[...], -slab_start + is_last * length, tiles + extra, near_table,
               source_table, None)


def pair_tile(tile, packet_ref, slab_start, weight_b, lists_ref, near_table, source_table, home_table,
              out_ref):
    slots = lists_ref.shape[0]
    at = pl.ds(pl.multiple_of(tile * TILE, TILE), TILE)
    home = home_table[tile]
    blank = jnp.zeros_like(home)
    rest = jnp.zeros((TILE - 2 * home.shape[0], 2 * TILE), jnp.float32)
    wide_home = jnp.concatenate(
        [jnp.concatenate([home, blank], axis=1), jnp.concatenate([blank, home], axis=1), rest], axis=0)
    lane = lax.broadcasted_iota(jnp.int32, (TILE, TILE), 1)
    total = jnp.zeros((32, 2 * TILE), jnp.float32)
    for slot in range(0, slots, 2):
        one, two = lists_ref[slot, tile], lists_ref[slot + 1, tile]
        near = jnp.where(lane < 32, near_table[one], near_table[two])
        source = jnp.concatenate([source_table[one], source_table[two]], axis=1)
        square = dot(near, wide_home)
        inverse = lax.rsqrt(square)
        tail = (1.0 - lax.erf(square * inverse)) * inverse
        gauss = jnp.exp2(square * (-1.0 / math.log(2.0))) * (2.0 / math.sqrt(math.pi))
        radial = (tail + gauss) * (inverse * inverse)
        low = low_part(radial)
        both = jnp.concatenate(
            [jnp.concatenate([radial[:, :TILE], low[:, :TILE]], axis=1),
             jnp.concatenate([radial[:, TILE:], low[:, TILE:]], axis=1)], axis=0)
        total = total + dot(source, both)
    sums = total[:, :TILE] + total[:, TILE:]
    sums = sums[0:8] + sums[8:16] + sums[16:24]
    rows = packet_ref[:, at]
    local = jnp.concatenate([rows[0:1] - (slab_start + 0.5), rows[1:3] - 4.0], axis=0)
    scale = beta ** 3
    part_a = local * sums[0:1] - sums[1:4]
    part_b = local * sums[4:5] - sums[5:8]
    out_ref[:, at] = (
        ((1.0 - weight_b) * scale) * rows[3:4] * part_a + (weight_b * scale) * rows[4:5] * part_b)


VM = pl.BlockSpec(memory_space=pltpu.VMEM)
SM = pl.BlockSpec(memory_space=pltpu.SMEM)
params = pltpu.CompilerParams(vmem_limit_bytes=VMEM_LIMIT)


def f32(*shape):
    return jax.ShapeDtypeStruct(shape, jnp.float32)


def spread_atoms(chunk, charge_refs, base_ref, spline_ref, spread_out, grid_sum):
    order, _, full_y, full_z = spread_out.shape
    grid_sum[...] = jnp.zeros_like(grid_sum)

    def body(step, carry):
        at = pl.ds(pl.multiple_of(step * chunk, chunk), chunk)
        base = base_ref[:, at]
        weights = spline_ref[:, :, at]
        rows_y, = spline_columns(base[1:2], [[weights[1, o][None] for o in range(order)]], full_y)
        rows_z, = spline_columns(base[2:3], [[weights[2, o][None] for o in range(order)]], full_z)
        left = jnp.concatenate([ref[:, at] * rows_y for ref in charge_refs], axis=0)
        right = jnp.concatenate([weights[0, layer][None] * rows_z for layer in range(order)], axis=0)
        high = dot(jnp.concatenate([left, low_part(left)], axis=0), right, ((1,), (1,)))
        rest = dot(left, low_part(right), ((1,), (1,)))
        grid_sum[...] += high[:2 * full_y] + high[2 * full_y:] + rest
        return carry

    lax.fori_loop(0, base_ref.shape[1] // chunk, body, 0)
    for state in range(2):
        for layer in range(order):
            spread_out[layer, state] = grid_sum[state * full_y:(state + 1) * full_y,
                                                layer * full_z:(layer + 1) * full_z]


def gather_prepare(chunk, weight_b, charge_refs, base_ref, spline_ref, slope_ref, rows_y_ref,
                   slope_y_ref, wide_ref, low_ref, first, last):
    full_y = rows_y_ref.shape[0]
    order = spline_ref.shape[1]

    def body(step, carry):
        at = pl.ds(pl.multiple_of(step * chunk, chunk), chunk)
        twice = pl.ds(pl.multiple_of(step * 2 * chunk, 2 * chunk), 2 * chunk)
        base = base_ref[:, at]
        weights = spline_ref[:, :, at]
        slopes = slope_ref[:, :, at]

        def both(axis):
            return spline_columns(
                base[axis:axis + 1],
                [[table[axis, o][None] for o in range(order)] for table in (weights, slopes)],
                full_y)

        rows_y_ref[:, at], slope_y_ref[:, at] = both(1)
        stacked_z = jnp.concatenate(both(2), axis=1)
        scales = [(weight_b - 1.0) * charge_refs[0][:, at], -weight_b * charge_refs[1][:, at]]
        wide = jnp.concatenate(
            [jnp.concatenate([scale, scale], axis=1) * stacked_z for scale in scales], axis=0)
        wide_ref[:, twice] = wide
        low_ref[:, twice] = low_part(wide)
        return carry

    lax.fori_loop(first, last, body, 0)


def gather_atoms(chunk, spline_ref, slope_ref, plane_ref, rows_y_ref, slope_y_ref, wide_ref, low_ref,
                 out_ref, planes):
    order, _, full_y, full_z = plane_ref.shape
    height = order * full_y
    for state in range(2):
        for layer in range(order):
            value = plane_ref[layer, state]
            lanes = slice(state * full_z, (state + 1) * full_z)
            planes[layer * full_y:(layer + 1) * full_y, lanes] = value
            planes[height + layer * full_y:height + (layer + 1) * full_y, lanes] = low_part(value)

    def body(step, carry):
        at = pl.ds(pl.multiple_of(step * chunk, chunk), chunk)
        twice = pl.ds(pl.multiple_of(step * 2 * chunk, 2 * chunk), 2 * chunk)
        weights = spline_ref[0, :, at]
        slopes = slope_ref[0, :, at]
        rows_y, slope_y = rows_y_ref[:, at], slope_y_ref[:, at]
        high = dot(planes[...], wide_ref[:, twice])
        rest = dot(planes[:height, :], low_ref[:, twice])
        sums = [jnp.zeros((8, chunk), jnp.float32) for _ in range(3)]
        for layer in range(order):
            part = slice(layer * full_y, (layer + 1) * full_y)
            again = slice(height + layer * full_y, height + (layer + 1) * full_y)
            sampled = high[part] + high[again] + rest[part]
            plain, sloped = sampled[:, :chunk], sampled[:, chunk:]
            plain_x, slope_x = weights[layer:layer + 1], slopes[layer:layer + 1]
            sums[0] = sums[0] + slope_x * sum_tiles(plain * rows_y)
            sums[1] = sums[1] + plain_x * sum_tiles(plain * slope_y)
            sums[2] = sums[2] + plain_x * sum_tiles(sloped * rows_y)
        for axis in range(3):
            out_ref[axis:axis + 1, at] = jnp.sum(sums[axis], axis=0, keepdims=True)
        return carry

    lax.fori_loop(0, spline_ref.shape[2] // chunk, body, 0)

MESH = pl.DeviceIdType.MESH
ATOMS_AT_ONCE = 512


def each(first, last, body, width):
    head = (last - first) % width
    for step in range(head):
        body(first + step)

    def block(index, carry):
        for step in range(width):
            body(first + head + index * width + step)
        return carry

    lax.fori_loop(0, (last - first - head) // width, block, 0)


def pick_ghosts(chunk, packet_ref, ghost_ref, ghost_out):
    height, atoms = packet_ref.shape
    ghosts = ghost_ref.shape[1]

    def pick(step, carry):
        at = pl.ds(pl.multiple_of(step * chunk, chunk), chunk)
        parts = jnp.concatenate(three_parts(packet_ref[:, at]), axis=0)
        ids = lax.broadcasted_iota(jnp.int32, (chunk, ghosts), 0) + step * chunk
        results = []
        for side in range(2):
            chosen = jnp.where(ids == ghost_ref[side:side + 1, :], 1.0, 0.0)
            results.append(carry[side] + dot(parts, chosen))
        return tuple(results)

    start = jnp.zeros((3 * height, ghosts), jnp.float32)
    sides = lax.fori_loop(0, atoms // chunk, pick, (start, start))
    for side, value in enumerate(sides):
        ghost_out[side] = value[:height] + value[height:2 * height] + value[2 * height:]


def step_kernel(group, windows, scale, coupling_ref, lists_ref, *refs):
    inputs, (out_ref, real_ref), held, refs = refs[:10], refs[10:12], refs[12:22], refs[22:]
    (charge_a_ref, charge_b_ref, base_ref, spline_ref, position_ref, ghost_ref, slope_ref, table_ref,
     tablet_ref, influence_ref) = held
    (input_sem, rows_y, slope_y, wide_z, low_z, packet_ref, grid_sum, planes, spread_out, near_in, far_out, far_in, ghost_out, ghost_in, there_out, there_in, back_out, back_in,
     plane_in, near_table, source_table, home_table,
     near_send, near_recv, far_send, far_recv, ghost_send, ghost_recv, row_send, row_recv, row_own,
     plane_send, plane_recv) = refs
    loads = [pltpu.make_async_copy(src, dst, input_sem.at[index])
             for index, (src, dst) in enumerate(zip(inputs, held))]
    for copy in loads:
        copy.start()
    me = lax.axis_index("px")
    order, _, full_y, full_z = spread_out.shape
    full_x = influence_ref.shape[0]
    tiles = lists_ref.shape[1]
    slab_start = me.astype(jnp.float32)

    def other(steps):
        return {"px": lax.rem(me + (steps + group), group)}

    barrier = pltpu.get_barrier_semaphore()

    def greet(steps):
        pl.semaphore_signal(barrier, inc=1, device_id=other(steps), device_id_type=MESH)

    with jax.named_scope("greet"):
        each(1, group, greet, 14)

    charge_refs = (charge_a_ref, charge_b_ref)
    for copy in loads[:4]:
        copy.wait()
    with jax.named_scope("spread"):
        spread_atoms(2048, charge_refs, base_ref, spline_ref, spread_out, grid_sum)

    with jax.named_scope("barrier_wait"):
        pl.semaphore_wait(barrier, group - 1)

    odd = lax.rem(me, 2)
    partner = other(1 - 2 * odd)

    def carry_to(device, src, dst, sends, recvs, at):
        return pltpu.make_async_remote_copy(
            src_ref=src, dst_ref=dst, send_sem=sends.at[at], recv_sem=recvs.at[at],
            device_id=device, device_id_type=MESH)

    third = [carry_to(other(1), spread_out.at[3, s], near_in.at[1, s], near_send, near_recv, 2 + s)
             for s in range(2)]
    first = [carry_to(partner, spread_out.at[1, s], near_in.at[0, s], near_send, near_recv, s)
             for s in range(2)]
    far = [carry_to(other(2), far_out.at[s], far_in.at[s], far_send, far_recv, s) for s in range(2)]
    visits = [carry_to(other(1 - 2 * side), ghost_out.at[side], ghost_in.at[side], ghost_send,
                       ghost_recv, side) for side in range(2)]
    for copy in third + first:
        copy.start()
    for copy in loads[4:]:
        copy.wait()
    with jax.named_scope("pick"):
        packet_ref[0:3, :] = position_ref[...]
        packet_ref[3:4, :] = charge_a_ref[...]
        packet_ref[4:5, :] = charge_b_ref[...]
        packet_ref[5:8, :] = jnp.zeros_like(position_ref)
        pick_ghosts(512, packet_ref, ghost_ref, ghost_out)
    prepare = functools.partial(gather_prepare, ATOMS_AT_ONCE, coupling_ref[0], charge_refs, base_ref,
                                spline_ref, slope_ref, rows_y, slope_y, wide_z, low_z)
    with jax.named_scope("prepare_a"):
        prepare(0, 2)
    with jax.named_scope("wait_near"):
        for s in range(2):
            first[s].wait()
            third[s].wait()
            far_out[s] = spread_out[2, s] + near_in[1, s] + jnp.where(odd == 0, near_in[0, s], 0.0)
            far[s].start()
    for copy in visits:
        copy.start()
    with jax.named_scope("pair_own"):
        pair_own(slab_start, packet_ref, near_table, source_table, home_table)
    with jax.named_scope("prepare_b"):
        prepare(2, 5)
    with jax.named_scope("wait_far"):
        for copy in far:
            copy.wait()

    def swap_rows(out_rows, in_rows, which):
        def row_to(steps):
            return pltpu.make_async_remote_copy(
                src_ref=out_rows.at[lax.rem(me + steps, group)], dst_ref=in_rows.at[me],
                send_sem=row_send.at[which], recv_sem=row_recv.at[which],
                device_id=other(steps), device_id_type=MESH)

        own = pltpu.make_async_copy(out_rows.at[me], in_rows.at[me], row_own.at[which])
        own.start()
        half = group // 2
        row_to(half).start()

        def send(steps):
            row_to(half - steps).start()
            row_to(half + steps).start()

        each(1, half, send, 7)

        def finish():
            own.wait()
            every = pltpu.make_async_remote_copy(
                src_ref=out_rows.at[pl.ds(0, group - 1)], dst_ref=in_rows.at[pl.ds(0, group - 1)],
                send_sem=row_send.at[which], recv_sem=row_recv.at[which],
                device_id=other(half), device_id_type=MESH)
            every.wait()

        return finish

    def pairs(first, last):
        def body(tile, carry):
            pair_tile(tile, packet_ref, slab_start, coupling_ref[0], lists_ref, near_table,
                      source_table, home_table, real_ref)
            return carry

        lax.fori_loop(first, last, body, 0, unroll=4)

    table, tablet = table_ref[...], tablet_ref[...]
    value = spread_out[0] + far_in[...] + jnp.where(odd == 0, 0.0, near_in[0])
    rows = dot3(jnp.concatenate([value[0], value[1]], axis=1), table)
    columns = dot3(tablet, jnp.concatenate([rows[:, :full_z], rows[:, full_z:]], axis=0))
    there_out[:, 0, :] = columns[:full_y]
    there_out[:, 1, :] = columns[full_y:]
    with jax.named_scope("send_there"):
        finish = swap_rows(there_out, there_in, 0)

    for copy in visits:
        copy.wait()
    is_first = jnp.where(me == 0, 1.0, 0.0)
    is_last = jnp.where(me == group - 1, 1.0, 0.0)
    pair_ghosts(slab_start, float(full_x), ghost_in.at[0], ghost_in.at[1], is_first, is_last, tiles,
                near_table, source_table)
    with jax.named_scope("pairs_a"):
        pairs(0, windows[0])
    with jax.named_scope("prepare_c"):
        prepare(5, base_ref.shape[1] // ATOMS_AT_ONCE)
    with jax.named_scope("wait_there"):
        finish()

    columns = dot3(tablet, jnp.concatenate([there_in[:, 0, :], there_in[:, 1, :]], axis=0))
    gain = influence_ref[...] * scale
    columns = dot3(table, columns * jnp.concatenate([gain, gain], axis=0))
    back_out[:, 0, :] = columns[:full_x]
    back_out[:, 1, :] = columns[full_x:]
    with jax.named_scope("send_back"):
        finish = swap_rows(back_out, back_in, 1)
    with jax.named_scope("pairs_b"):
        pairs(windows[0], windows[1])
    with jax.named_scope("wait_back"):
        finish()

    columns = dot3(table, jnp.concatenate([back_in[:, 0, :], back_in[:, 1, :]], axis=0))
    rows = dot3(jnp.concatenate([columns[:full_y], columns[full_y:]], axis=1), tablet)
    plane_in[0, 0] = rows[:, :full_z]
    plane_in[0, 1] = rows[:, full_z:]
    lend_two = [carry_to(other(-2), plane_in.at[0, s], plane_in.at[2, s], plane_send, plane_recv, s)
                for s in range(2)]
    lend_three = [carry_to(other(-1), plane_in.at[2, s], plane_in.at[3, s], plane_send, plane_recv,
                           2 + s) for s in range(2)]
    lend_one, pass_one = (
        [carry_to(partner, plane_in.at[at, s], plane_in.at[1, s], plane_send, plane_recv, 4 + s)
         for s in range(2)] for at in (0, 2))
    for copy in lend_two:
        copy.start()

    @pl.when(odd == 1)
    def _():
        for copy in lend_one:
            copy.start()

    with jax.named_scope("pairs_c"):
        pairs(windows[1], windows[2])
    with jax.named_scope("wait_two"):
        for s in range(2):
            lend_two[s].wait()
            lend_three[s].start()

            @pl.when(odd == 0)
            def _():
                pass_one[s].start()

    with jax.named_scope("pairs_d"):
        pairs(windows[2], tiles)
    with jax.named_scope("wait_three"):
        for copy in lend_three + lend_one:
            copy.wait()
    with jax.named_scope("gather"):
        gather_atoms(ATOMS_AT_ONCE, spline_ref, slope_ref, plane_in, rows_y, slope_y, wide_z, low_z,
                     out_ref, planes)


def run_step(group, coupling, lists, charge_a, charge_b, positions, grid_base, spline, slope, ghosts,
             influence):
    order = spline.shape[1]
    full_x, full_z = influence.shape
    full_y = group
    atoms = positions.shape[1]
    tiles = lists.shape[1]
    visitors = ghosts.shape[1]
    every = tiles + 2 * (visitors // TILE)
    plane = (2, full_y, full_z)
    table, tablet = (jnp.asarray(value) for value in dft_tables(full_x))
    windows = (tiles * 3 // 8, tiles * 6 // 8, tiles * 7 // 8)
    inputs = (charge_a, charge_b, grid_base, spline, positions, ghosts, slope, table, tablet, influence)
    return pl.pallas_call(
        functools.partial(step_kernel, group, windows, 1.0 / (full_x * full_y * full_z)),
        out_shape=[f32(3, atoms)] * 2,
        in_specs=[SM] * 2 + [pl.BlockSpec(memory_space=pl.ANY)] * len(inputs),
        out_specs=[VM] * 2,
        scratch_shapes=[pltpu.VMEM(value.shape, value.dtype) for value in inputs] + [
            pltpu.SemaphoreType.DMA((len(inputs),)),
            pltpu.VMEM((full_y, atoms), jnp.float32),
            pltpu.VMEM((full_y, atoms), jnp.float32),
            pltpu.VMEM((2 * full_z, 2 * atoms), jnp.float32),
            pltpu.VMEM((2 * full_z, 2 * atoms), jnp.float32),
            pltpu.VMEM((8, atoms), jnp.float32),
            pltpu.VMEM((2 * full_y, order * full_z), jnp.float32),
            pltpu.VMEM((2 * order * full_y, 2 * full_z), jnp.float32),
            pltpu.VMEM((order, *plane), jnp.float32),
            pltpu.VMEM((2, *plane), jnp.float32),
            pltpu.VMEM(plane, jnp.float32),
            pltpu.VMEM(plane, jnp.float32),
            pltpu.VMEM((2, 8, visitors), jnp.float32),
            pltpu.VMEM((2, 8, visitors), jnp.float32),
            pltpu.VMEM((group, 2, full_z), jnp.float32),
            pltpu.VMEM((group, 2, full_z), jnp.float32),
            pltpu.VMEM((group, 2, full_z), jnp.float32),
            pltpu.VMEM((group, 2, full_z), jnp.float32),
            pltpu.VMEM((order, *plane), jnp.float32),
            pltpu.VMEM((every, TILE, TILE), jnp.float32),
            pltpu.VMEM((every, 32, TILE), jnp.float32),
            pltpu.VMEM((tiles, 32, TILE), jnp.float32),
            pltpu.SemaphoreType.DMA((4,)),
            pltpu.SemaphoreType.DMA((4,)),
            pltpu.SemaphoreType.DMA((2,)),
            pltpu.SemaphoreType.DMA((2,)),
            pltpu.SemaphoreType.DMA((2,)),
            pltpu.SemaphoreType.DMA((2,)),
            pltpu.SemaphoreType.DMA((2,)),
            pltpu.SemaphoreType.DMA((2,)),
            pltpu.SemaphoreType.DMA((2,)),
            pltpu.SemaphoreType.DMA((6,)),
            pltpu.SemaphoreType.DMA((6,)),
        ],
        compiler_params=pltpu.CompilerParams(
            vmem_limit_bytes=VMEM_LIMIT, collective_id=0, has_side_effects=True),
    )(coupling, lists, *inputs)


def per_device(charge_a, charge_b, coupling, positions, grid_base, spline, spline_slope, influence,
               pair_tiles, ghost_lists):
    group = lax.axis_size("px")
    reciprocal, real_space = run_step(
        group, coupling, pair_tiles.T, charge_a[None], charge_b[None], positions, grid_base, spline,
        spline_slope, ghost_lists, influence[:, 0])
    return reciprocal + real_space


def solution(mesh):
    placed = (
        P(("win", "px")),
        P(("win", "px")),
        P("win"),
        P(None, ("win", "px")),
        P(None, ("win", "px")),
        P(None, None, ("win", "px")),
        P(None, None, ("win", "px")),
        P(None, "px", None),
        P(("win", "px"), None),
        P(None, ("win", "px")),
    )
    return jax.shard_map(
        per_device, mesh=mesh, in_specs=placed, out_specs=P(None, ("win", "px")), check_vma=False
    )
```

time: 109 us -> 84 us (0.77)
  Pallas kernels: 105 us -> 81.7 us
  local copies, waits for them, and re-layouts: 1.47 us -> 0 us
    pallas_call x1 -> x0, Pallas kernels: 17.5 us -> none  [run_gather(): pl.pallas_call(functools.partial(gather_kernel, chunk, order), out_shape=...]
    pallas_call x1, Pallas kernels: 87.7 us -> 81.7 us  [run_step(): pl.pallas_call(functools.partial(step_kernel, group, windows, 1.0 / (full...]
    add x0 -> x1, other arithmetic: none -> 1.52 us  [per_device(): return reciprocal + real_space]
    unnamed x7 -> x0, local copies, waits for them, and re-layouts: 1.39 us -> none
where the time goes in v3:
time: 84 us; the launch traced here: 83.9 us
  Pallas kernels  81.7 us (97%)
  other arithmetic  1.52 us (2%)
    pallas_call x1, Pallas kernels, run_step(): pl.pallas_call(functools.partial(step_kernel, group, windows, 1.0 / (full...  81.7 us

profile of v3, /device:TPU:33, one launch (start us, length us, event | category | flops | bytes accessed | tf_op | source)
XLA Modules:
  0.0 83.9 jit_solution(1184088460944141806)
XLA Ops:
  0.7 81.7 %shard_map.118 = (f32[3,4096]{1,0:T(4,128)}, f32[3,4096]{1,0:T(4,128)}) custom-call(f32[1]{0:T(128)S(6)} %copy.13.coupling_ref, s32[12,32]{1,0:T(8,128)} %bitcast.7, f32[1,4096]{1,0:T(1,128)} %bitcast.5, f32[1,4096]{1,0:T(1,128)} %bitcast.6, s32[3,4096]{1,0:T(4,128)} %refs_2_.1, f32[3,4,4096]{2,1,0:T(4,128)} %refs_3_.1, f32[3,4096]{1,0:T(4,128)} %refs_4_.1, ...), custom_call_target="tpu_custom_call" | custom-call | tf_op jit(solution)/shard_map/pallas_call | solution.py:489
  82.3 1.5 %add.3 = f32[3,4096]{1,0:T(4,128)} add(f32[3,4096]{1,0:T(4,128)} %get-tuple-element.7, f32[3,4096]{1,0:T(4,128)} %get-tuple-element.8) | non-fusion elementwise | flops 12288 | bytes 147456 | tf_op jit(solution)/shard_map/add | solution.py:540

commit v4 on v3

--- a/solution.py
+++ b/solution.py
@@ -208,16 +208,18 @@
     lax.fori_loop(first, last, body, 0)
 
 
-def gather_atoms(chunk, spline_ref, slope_ref, plane_ref, rows_y_ref, slope_y_ref, wide_ref, low_ref,
-                 out_ref, planes):
-    order, _, full_y, full_z = plane_ref.shape
-    height = order * full_y
+def gather_layers(chunk, unroll, layers, before, spline_ref, slope_ref, plane_ref, rows_y_ref, slope_y_ref,
+                  wide_ref, low_ref, out_ref, planes):
+    _, _, full_y, full_z = plane_ref.shape
+    height = len(layers) * full_y
+    top = before * 2 * full_y
     for state in range(2):
-        for layer in range(order):
+        lanes = slice(state * full_z, (state + 1) * full_z)
+        for place, layer in enumerate(layers):
             value = plane_ref[layer, state]
-            lanes = slice(state * full_z, (state + 1) * full_z)
-            planes[layer * full_y:(layer + 1) * full_y, lanes] = value
-            planes[height + layer * full_y:height + (layer + 1) * full_y, lanes] = low_part(value)
+            first = top + place * full_y
+            planes[first:first + full_y, lanes] = value
+            planes[first + height:first + height + full_y, lanes] = low_part(value)
 
     def body(step, carry):
         at = pl.ds(pl.multiple_of(step * chunk, chunk), chunk)
@@ -225,12 +227,12 @@
         weights = spline_ref[0, :, at]
         slopes = slope_ref[0, :, at]
         rows_y, slope_y = rows_y_ref[:, at], slope_y_ref[:, at]
-        high = dot(planes[...], wide_ref[:, twice])
-        rest = dot(planes[:height, :], low_ref[:, twice])
+        high = dot(planes[top:top + 2 * height, :], wide_ref[:, twice])
+        rest = dot(planes[top:top + height, :], low_ref[:, twice])
         sums = [jnp.zeros((8, chunk), jnp.float32) for _ in range(3)]
-        for layer in range(order):
-            part = slice(layer * full_y, (layer + 1) * full_y)
-            again = slice(height + layer * full_y, height + (layer + 1) * full_y)
+        for place, layer in enumerate(layers):
+            part = slice(place * full_y, (place + 1) * full_y)
+            again = slice(height + place * full_y, height + (place + 1) * full_y)
             sampled = high[part] + high[again] + rest[part]
             plain, sloped = sampled[:, :chunk], sampled[:, chunk:]
             plain_x, slope_x = weights[layer:layer + 1], slopes[layer:layer + 1]
@@ -238,7 +240,10 @@
             sums[1] = sums[1] + plain_x * sum_tiles(plain * slope_y)
             sums[2] = sums[2] + plain_x * sum_tiles(sloped * rows_y)
         for axis in range(3):
-            out_ref[axis:axis + 1, at] = jnp.sum(sums[axis], axis=0, keepdims=True)
+            result = jnp.sum(sums[axis], axis=0, keepdims=True)
+            if before:
+                result = result + out_ref[axis:axis + 1, at]
+            out_ref[axis:axis + 1, at] = result
         return carry
 
     lax.fori_loop(0, spline_ref.shape[2] // chunk, body, 0)
@@ -280,13 +285,15 @@
         ghost_out[side] = value[:height] + value[height:2 * height] + value[2 * height:]
 
 
-def step_kernel(group, windows, scale, coupling_ref, lists_ref, *refs):
-    inputs, (out_ref, real_ref), held, refs = refs[:10], refs[10:12], refs[12:22], refs[22:]
-    (charge_a_ref, charge_b_ref, base_ref, spline_ref, position_ref, ghost_ref, slope_ref, table_ref,
-     tablet_ref, influence_ref) = held
-    (input_sem, rows_y, slope_y, wide_z, low_z, packet_ref, grid_sum, planes, spread_out, near_in, far_out, far_in, ghost_out, ghost_in, there_out, there_in, back_out, back_in,
+def step_kernel(group, scale, coupling_ref, lists_ref, *refs):
+    inputs, (out_ref, real_ref), held, refs = refs[:14], refs[14:16], refs[16:30], refs[30:]
+    (charge_a_ref, charge_b_ref, base_ref, spline_ref, position_ref, ghost_ref, slope_ref, influence_ref,
+     table_ref, tablet_ref, table_rows_ref, tablet_rows_ref, table_columns_ref, tablet_columns_ref) = held
+    (input_sem, rows_y, slope_y, wide_z, low_z, packet_ref, grid_sum, planes, spread_out, near_in, far_out, far_in, ghost_out, ghost_in, there_cross, there_out, there_in,
+     back_cross, back_out, back_in,
      plane_in, near_table, source_table, home_table,
-     near_send, near_recv, far_send, far_recv, ghost_send, ghost_recv, row_send, row_recv, row_own,
+     near_send, near_recv, far_send, far_recv, ghost_send, ghost_recv, cross_send, cross_recv, row_send, row_recv,
+     row_own,
      plane_send, plane_recv) = refs
     loads = [pltpu.make_async_copy(src, dst, input_sem.at[index])
              for index, (src, dst) in enumerate(zip(inputs, held))]
@@ -306,8 +313,19 @@
     def greet(steps):
         pl.semaphore_signal(barrier, inc=1, device_id=other(steps), device_id_type=MESH)
 
+    chips = group // 2
+    half = chips // 2
+
     with jax.named_scope("greet"):
-        each(1, group, greet, 14)
+        greet(2 * half)
+
+        def greet_both(steps):
+            greet(2 * (half - steps))
+            greet(2 * (half + steps))
+
+        each(1, half, greet_both, 5)
+        greet(1)
+        greet(-1)
 
     charge_refs = (charge_a_ref, charge_b_ref)
     for copy in loads[:4]:
@@ -316,7 +334,7 @@
         spread_atoms(2048, charge_refs, base_ref, spline_ref, spread_out, grid_sum)
 
     with jax.named_scope("barrier_wait"):
-        pl.semaphore_wait(barrier, group - 1)
+        pl.semaphore_wait(barrier, chips + 1)
 
     odd = lax.rem(me, 2)
     partner = other(1 - 2 * odd)
@@ -335,7 +353,7 @@
                        ghost_recv, side) for side in range(2)]
     for copy in third + first:
         copy.start()
-    for copy in loads[4:]:
+    for copy in loads[4:7]:
         copy.wait()
     with jax.named_scope("pick"):
         packet_ref[0:3, :] = position_ref[...]
@@ -345,51 +363,66 @@
         pick_ghosts(512, packet_ref, ghost_ref, ghost_out)
     prepare = functools.partial(gather_prepare, ATOMS_AT_ONCE, coupling_ref[0], charge_refs, base_ref,
                                 spline_ref, slope_ref, rows_y, slope_y, wide_z, low_z)
-    with jax.named_scope("prepare_a"):
-        prepare(0, 2)
+    for copy in visits:
+        copy.start()
     with jax.named_scope("wait_near"):
         for s in range(2):
             first[s].wait()
             third[s].wait()
             far_out[s] = spread_out[2, s] + near_in[1, s] + jnp.where(odd == 0, near_in[0, s], 0.0)
             far[s].start()
-    for copy in visits:
-        copy.start()
+    with jax.named_scope("prepare_a"):
+        prepare(0, 2)
     with jax.named_scope("pair_own"):
         pair_own(slab_start, packet_ref, near_table, source_table, home_table)
     with jax.named_scope("prepare_b"):
-        prepare(2, 5)
+        prepare(2, 6)
     with jax.named_scope("wait_far"):
         for copy in far:
             copy.wait()
 
-    def swap_rows(out_rows, in_rows, which):
+    chip = lax.div(me, 2)
+
+    def swap_rows(columns, cross, paired, in_rows, which):
+        upper, lower = columns[:group], columns[group:]
+        mine = jnp.where(odd == 0, upper, lower)
+        theirs = jnp.where(odd == 0, lower, upper)
+        for part in range(2):
+            rows_at = slice(part * chips, (part + 1) * chips)
+            cross[:, part, :] = theirs[rows_at]
+            paired[:, odd, part, :] = mine[rows_at]
+        over = carry_to(partner, cross, paired.at[:, odd], cross_send, cross_recv, which)
+        over.start()
+
         def row_to(steps):
             return pltpu.make_async_remote_copy(
-                src_ref=out_rows.at[lax.rem(me + steps, group)], dst_ref=in_rows.at[me],
+                src_ref=paired.at[lax.rem(chip + steps, chips)], dst_ref=in_rows.at[chip],
                 send_sem=row_send.at[which], recv_sem=row_recv.at[which],
-                device_id=other(steps), device_id_type=MESH)
-
-        own = pltpu.make_async_copy(out_rows.at[me], in_rows.at[me], row_own.at[which])
-        own.start()
-        half = group // 2
-        row_to(half).start()
+                device_id=other(2 * steps), device_id_type=MESH)
+
+        own = pltpu.make_async_copy(paired.at[chip], in_rows.at[chip], row_own.at[which])
 
         def send(steps):
             row_to(half - steps).start()
             row_to(half + steps).start()
 
-        each(1, half, send, 7)
+        def go():
+            over.wait()
+            own.start()
+            row_to(half).start()
+            each(1, half, send, 5)
 
         def finish():
             own.wait()
             every = pltpu.make_async_remote_copy(
-                src_ref=out_rows.at[pl.ds(0, group - 1)], dst_ref=in_rows.at[pl.ds(0, group - 1)],
+                src_ref=paired.at[pl.ds(0, chips - 1)], dst_ref=in_rows.at[pl.ds(0, chips - 1)],
                 send_sem=row_send.at[which], recv_sem=row_recv.at[which],
-                device_id=other(half), device_id_type=MESH)
+                device_id=other(2 * half), device_id_type=MESH)
             every.wait()
-
-        return finish
+            return jnp.concatenate(
+                [in_rows[:, side, part, :] for side in range(2) for part in range(2)], axis=0)
+
+        return go, finish
 
     def pairs(first, last):
         def body(tile, carry):
@@ -399,42 +432,41 @@
 
         lax.fori_loop(first, last, body, 0, unroll=4)
 
-    table, tablet = table_ref[...], tablet_ref[...]
+    for copy in loads[7:]:
+        copy.wait()
     value = spread_out[0] + far_in[...] + jnp.where(odd == 0, 0.0, near_in[0])
-    rows = dot3(jnp.concatenate([value[0], value[1]], axis=1), table)
-    columns = dot3(tablet, jnp.concatenate([rows[:, :full_z], rows[:, full_z:]], axis=0))
-    there_out[:, 0, :] = columns[:full_y]
-    there_out[:, 1, :] = columns[full_y:]
+    rows = dot3(jnp.concatenate([value[0], value[1]], axis=1), table_ref[...])
+    rows = jnp.concatenate([rows[:, :full_z], rows[:, full_z:]], axis=0)
+    go, finish = swap_rows(dot3(tablet_rows_ref[...], rows), there_cross, there_out, there_in, 0)
     with jax.named_scope("send_there"):
-        finish = swap_rows(there_out, there_in, 0)
-
-    for copy in visits:
-        copy.wait()
-    is_first = jnp.where(me == 0, 1.0, 0.0)
-    is_last = jnp.where(me == group - 1, 1.0, 0.0)
-    pair_ghosts(slab_start, float(full_x), ghost_in.at[0], ghost_in.at[1], is_first, is_last, tiles,
-                near_table, source_table)
+        go()
+    with jax.named_scope("ghosts"):
+        for copy in visits:
+            copy.wait()
+        is_first = jnp.where(me == 0, 1.0, 0.0)
+        is_last = jnp.where(me == group - 1, 1.0, 0.0)
+        pair_ghosts(slab_start, float(full_x), ghost_in.at[0], ghost_in.at[1], is_first, is_last,
+                    tiles, near_table, source_table)
     with jax.named_scope("pairs_a"):
-        pairs(0, windows[0])
+        pairs(0, tiles * 3 // 8)
     with jax.named_scope("prepare_c"):
-        prepare(5, base_ref.shape[1] // ATOMS_AT_ONCE)
+        prepare(6, base_ref.shape[1] // ATOMS_AT_ONCE)
     with jax.named_scope("wait_there"):
-        finish()
-
-    columns = dot3(tablet, jnp.concatenate([there_in[:, 0, :], there_in[:, 1, :]], axis=0))
+        columns = finish()
+
+    columns = dot3(tablet_columns_ref[...], columns)
     gain = influence_ref[...] * scale
-    columns = dot3(table, columns * jnp.concatenate([gain, gain], axis=0))
-    back_out[:, 0, :] = columns[:full_x]
-    back_out[:, 1, :] = columns[full_x:]
+    columns = dot3(table_rows_ref[...], columns * jnp.concatenate([gain, gain], axis=0))
+    go, finish = swap_rows(columns, back_cross, back_out, back_in, 1)
     with jax.named_scope("send_back"):
-        finish = swap_rows(back_out, back_in, 1)
+        go()
     with jax.named_scope("pairs_b"):
-        pairs(windows[0], windows[1])
+        pairs(tiles * 3 // 8, tiles)
     with jax.named_scope("wait_back"):
-        finish()
-
-    columns = dot3(table, jnp.concatenate([back_in[:, 0, :], back_in[:, 1, :]], axis=0))
-    rows = dot3(jnp.concatenate([columns[:full_y], columns[full_y:]], axis=1), tablet)
+        columns = finish()
+
+    columns = dot3(table_columns_ref[...], columns)
+    rows = dot3(jnp.concatenate([columns[:full_y], columns[full_y:]], axis=1), tablet_ref[...])
     plane_in[0, 0] = rows[:, :full_z]
     plane_in[0, 1] = rows[:, full_z:]
     lend_two = [carry_to(other(-2), plane_in.at[0, s], plane_in.at[2, s], plane_send, plane_recv, s)
@@ -452,8 +484,12 @@
         for copy in lend_one:
             copy.start()
 
-    with jax.named_scope("pairs_c"):
-        pairs(windows[1], windows[2])
+    def gather(layers, before):
+        gather_layers(ATOMS_AT_ONCE, 4 // len(layers), layers, before, spline_ref, slope_ref, plane_in,
+                      rows_y, slope_y, wide_z, low_z, out_ref, planes)
+
+    with jax.named_scope("gather_a"):
+        gather((0,), 0)
     with jax.named_scope("wait_two"):
         for s in range(2):
             lend_two[s].wait()
@@ -463,14 +499,13 @@
             def _():
                 pass_one[s].start()
 
-    with jax.named_scope("pairs_d"):
-        pairs(windows[2], tiles)
+    with jax.named_scope("gather_b"):
+        gather((2,), 1)
     with jax.named_scope("wait_three"):
         for copy in lend_three + lend_one:
             copy.wait()
-    with jax.named_scope("gather"):
-        gather_atoms(ATOMS_AT_ONCE, spline_ref, slope_ref, plane_in, rows_y, slope_y, wide_z, low_z,
-                     out_ref, planes)
+    with jax.named_scope("gather_c"):
+        gather((1, 3), 2)
 
 
 def run_step(group, coupling, lists, charge_a, charge_b, positions, grid_base, spline, slope, ghosts,
@@ -483,11 +518,15 @@
     visitors = ghosts.shape[1]
     every = tiles + 2 * (visitors // TILE)
     plane = (2, full_y, full_z)
-    table, tablet = (jnp.asarray(value) for value in dft_tables(full_x))
-    windows = (tiles * 3 // 8, tiles * 6 // 8, tiles * 7 // 8)
-    inputs = (charge_a, charge_b, grid_base, spline, positions, ghosts, slope, table, tablet, influence)
+    tables = dft_tables(full_x)
+    order_of = np.arange(full_x)
+    sides = [order_of[side::2] + part * full_x for side in range(2) for part in range(2)]
+    split = np.concatenate(sides)
+    tables = tables + tuple(value[split] for value in tables) + tuple(value[:, split] for value in tables)
+    inputs = (charge_a, charge_b, grid_base, spline, positions, ghosts, slope, influence,
+              *(jnp.asarray(value) for value in tables))
     return pl.pallas_call(
-        functools.partial(step_kernel, group, windows, 1.0 / (full_x * full_y * full_z)),
+        functools.partial(step_kernel, group, 1.0 / (full_x * full_y * full_z)),
         out_shape=[f32(3, atoms)] * 2,
         in_specs=[SM] * 2 + [pl.BlockSpec(memory_space=pl.ANY)] * len(inputs),
         out_specs=[VM] * 2,
@@ -506,25 +545,13 @@
             pltpu.VMEM(plane, jnp.float32),
             pltpu.VMEM((2, 8, visitors), jnp.float32),
             pltpu.VMEM((2, 8, visitors), jnp.float32),
-            pltpu.VMEM((group, 2, full_z), jnp.float32),
-            pltpu.VMEM((group, 2, full_z), jnp.float32),
-            pltpu.VMEM((group, 2, full_z), jnp.float32),
-            pltpu.VMEM((group, 2, full_z), jnp.float32),
+            *[pltpu.VMEM((group // 2, *sides, 2, full_z), jnp.float32)
+              for sides in ((), (2,), (2,)) * 2],
             pltpu.VMEM((order, *plane), jnp.float32),
             pltpu.VMEM((every, TILE, TILE), jnp.float32),
             pltpu.VMEM((every, 32, TILE), jnp.float32),
             pltpu.VMEM((tiles, 32, TILE), jnp.float32),
-            pltpu.SemaphoreType.DMA((4,)),
-            pltpu.SemaphoreType.DMA((4,)),
-            pltpu.SemaphoreType.DMA((2,)),
-            pltpu.SemaphoreType.DMA((2,)),
-            pltpu.SemaphoreType.DMA((2,)),
-            pltpu.SemaphoreType.DMA((2,)),
-            pltpu.SemaphoreType.DMA((2,)),
-            pltpu.SemaphoreType.DMA((2,)),
-            pltpu.SemaphoreType.DMA((2,)),
-            pltpu.SemaphoreType.DMA((6,)),
-            pltpu.SemaphoreType.DMA((6,)),
+            *[pltpu.SemaphoreType.DMA((count,)) for count in (4, 4, 2, 2, 2, 2, 2, 2, 2, 2, 2, 6, 6)],
         ],
         compiler_params=pltpu.CompilerParams(
             vmem_limit_bytes=VMEM_LIMIT, collective_id=0, has_side_effects=True),

time: 84 us -> 81.4 us (0.969)
  Pallas kernels: 81.7 us -> 79 us
    pallas_call x1, Pallas kernels: 81.7 us -> 79 us  [run_step(): pl.pallas_call(functools.partial(step_kernel, group, 1.0 / (full_x * full...]
where the time goes in v4:
time: 81.4 us; the launch traced here: 81.2 us
  Pallas kernels  79 us (97%)
  other arithmetic  1.52 us (2%)
    pallas_call x1, Pallas kernels, run_step(): pl.pallas_call(functools.partial(step_kernel, group, 1.0 / (full_x * full...  79 us

profile of v4, /device:TPU:33, one launch (start us, length us, event | category | flops | bytes accessed | tf_op | source)
XLA Modules:
  0.0 81.2 jit_solution(3510143983001073491)
XLA Ops:
  0.7 79.0 %shard_map.154 = (f32[3,4096]{1,0:T(4,128)}, f32[3,4096]{1,0:T(4,128)}) custom-call(f32[1]{0:T(128)S(6)} %copy.17.coupling_ref, s32[12,32]{1,0:T(8,128)} %bitcast.7, f32[1,4096]{1,0:T(1,128)} %bitcast.5, f32[1,4096]{1,0:T(1,128)} %bitcast.6, s32[3,4096]{1,0:T(4,128)} %refs_2_.1, f32[3,4,4096]{2,1,0:T(4,128)} %refs_3_.1, f32[3,4096]{1,0:T(4,128)} %refs_4_.1, ...), custom_call_target="tpu_custom_call" | custom-call | tf_op jit(solution)/shard_map/pallas_call | solution.py:528
  79.7 1.5 %add.3 = f32[3,4096]{1,0:T(4,128)} add(f32[3,4096]{1,0:T(4,128)} %get-tuple-element.7, f32[3,4096]{1,0:T(4,128)} %get-tuple-element.8) | non-fusion elementwise | flops 12288 | bytes 147456 | tf_op jit(solution)/shard_map/add | solution.py:567

commit v5 on v4

--- a/solution.py
+++ b/solution.py
@@ -246,7 +246,7 @@
             out_ref[axis:axis + 1, at] = result
         return carry
 
-    lax.fori_loop(0, spline_ref.shape[2] // chunk, body, 0)
+    lax.fori_loop(0, spline_ref.shape[2] // chunk, body, 0, unroll=unroll)
 
 MESH = pl.DeviceIdType.MESH
 ATOMS_AT_ONCE = 512
@@ -448,7 +448,7 @@
         pair_ghosts(slab_start, float(full_x), ghost_in.at[0], ghost_in.at[1], is_first, is_last,
                     tiles, near_table, source_table)
     with jax.named_scope("pairs_a"):
-        pairs(0, tiles * 3 // 8)
+        pairs(0, tiles // 2)
     with jax.named_scope("prepare_c"):
         prepare(6, base_ref.shape[1] // ATOMS_AT_ONCE)
     with jax.named_scope("wait_there"):
@@ -461,7 +461,7 @@
     with jax.named_scope("send_back"):
         go()
     with jax.named_scope("pairs_b"):
-        pairs(tiles * 3 // 8, tiles)
+        pairs(tiles // 2, tiles)
     with jax.named_scope("wait_back"):
         columns = finish()
 

time: 81.4 us -> 80 us (0.983)
  Pallas kernels: 79 us -> 77.6 us
    pallas_call x1, Pallas kernels: 79 us -> 77.6 us  [run_step(): pl.pallas_call(functools.partial(step_kernel, group, 1.0 / (full_x * full...]
where the time goes in v5:
time: 80 us; the launch traced here: 79.8 us
  Pallas kernels  77.6 us (97%)
  other arithmetic  1.52 us (2%)
    pallas_call x1, Pallas kernels, run_step(): pl.pallas_call(functools.partial(step_kernel, group, 1.0 / (full_x * full...  77.6 us

profile of v5, /device:TPU:33, one launch (start us, length us, event | category | flops | bytes accessed | tf_op | source)
XLA Modules:
  0.0 79.8 jit_solution(6433167182785592739)
XLA Ops:
  0.7 77.6 %shard_map.154 = (f32[3,4096]{1,0:T(4,128)}, f32[3,4096]{1,0:T(4,128)}) custom-call(f32[1]{0:T(128)S(6)} %copy.17.coupling_ref, s32[12,32]{1,0:T(8,128)} %bitcast.7, f32[1,4096]{1,0:T(1,128)} %bitcast.5, f32[1,4096]{1,0:T(1,128)} %bitcast.6, s32[3,4096]{1,0:T(4,128)} %refs_2_.1, f32[3,4,4096]{2,1,0:T(4,128)} %refs_3_.1, f32[3,4096]{1,0:T(4,128)} %refs_4_.1, ...), custom_call_target="tpu_custom_call" | custom-call | tf_op jit(solution)/shard_map/pallas_call | solution.py:528
  78.3 1.5 %add.3 = f32[3,4096]{1,0:T(4,128)} add(f32[3,4096]{1,0:T(4,128)} %get-tuple-element.7, f32[3,4096]{1,0:T(4,128)} %get-tuple-element.8) | non-fusion elementwise | flops 12288 | bytes 147456 | tf_op jit(solution)/shard_map/add | solution.py:567

commit v6 on v5

--- a/solution.py
+++ b/solution.py
@@ -430,7 +430,7 @@
                       source_table, home_table, real_ref)
             return carry
 
-        lax.fori_loop(first, last, body, 0, unroll=4)
+        lax.fori_loop(first, last, body, 0, unroll=8)
 
     for copy in loads[7:]:
         copy.wait()

time: 80 us -> 80 us (level)
  no operation moved by 1% of the time
where the time goes in v6:
time: 80 us; the launch traced here: 79.8 us
  Pallas kernels  77.6 us (97%)
  other arithmetic  1.52 us (2%)
    pallas_call x1, Pallas kernels, run_step(): pl.pallas_call(functools.partial(step_kernel, group, 1.0 / (full_x * full...  77.6 us

profile of v6, /device:TPU:33, one launch (start us, length us, event | category | flops | bytes accessed | tf_op | source)
XLA Modules:
  0.0 79.8 jit_solution(7624486595503507145)
XLA Ops:
  0.7 77.6 %shard_map.154 = (f32[3,4096]{1,0:T(4,128)}, f32[3,4096]{1,0:T(4,128)}) custom-call(f32[1]{0:T(128)S(6)} %copy.17.coupling_ref, s32[12,32]{1,0:T(8,128)} %bitcast.7, f32[1,4096]{1,0:T(1,128)} %bitcast.5, f32[1,4096]{1,0:T(1,128)} %bitcast.6, s32[3,4096]{1,0:T(4,128)} %refs_2_.1, f32[3,4,4096]{2,1,0:T(4,128)} %refs_3_.1, f32[3,4096]{1,0:T(4,128)} %refs_4_.1, ...), custom_call_target="tpu_custom_call" | custom-call | tf_op jit(solution)/shard_map/pallas_call | solution.py:528
  78.3 1.5 %add.3 = f32[3,4096]{1,0:T(4,128)} add(f32[3,4096]{1,0:T(4,128)} %get-tuple-element.7, f32[3,4096]{1,0:T(4,128)} %get-tuple-element.8) | non-fusion elementwise | flops 12288 | bytes 147456 | tf_op jit(solution)/shard_map/add | solution.py:567
